TPU v7x, 128 devices: a whole 4x4x4 slice. The times are simulated.
128 devices in a mesh: dp: 2 (over z_hi), row: 4 (over x), col: 16 (over z_lo, y, core).
Axes of the slice: x: 4, y: 4, z: 4 (z_hi: 2, z_lo: 2; z = z_hi * 2 + z_lo), core: 2. Of those that a mesh axis runs over, the one named last changes fastest.
Arguments:
- stash_codes: int32 [4096, 4096], P(('dp', 'col'), 'row'), may hold values from 0 to 3
- stash_scales: int32 [4096, 32], P(('dp', 'col'), 'row'), may hold values from 1 to 8
- pad_mask: int32 [4096], P(('dp', 'col')), may hold values 0 or 1
- cotangent: bfloat16 [4096, 4096], P(('dp', 'col'), 'row'), may hold values from -3 to 3
- w_gate: bfloat16 [4096, 10240], P('row', 'col'), may hold values from -0.09375 to 0.09375
- w_up: bfloat16 [4096, 10240], P('row', 'col'), may hold values from -0.09375 to 0.09375
- w_out: bfloat16 [4096, 10240], P('row', 'col'), may hold values from -0.09375 to 0.09375
Outputs:
- input_grad: float32 [4096, 4096], P(('dp', 'col'), 'row')
- gate_weight_grad: float32 [4096, 10240], P('row', 'col')
- up_weight_grad: float32 [4096, 10240], P('row', 'col')
- out_weight_grad: float32 [4096, 10240], P('row', 'col')
All inputs are finite; a program needn't handle non-finite values. No bound on the sum of `pad_mask` on one device may be relied on, other than what follows from the above.
Results may differ from a plain program's by a relative error of at most 0.0029.
Values may be sent and summed in bfloat16 or wider, within the bound.
A program may use at most 128 MiB of HBM per device.

v0:
```python
import jax
import jax.numpy as jnp
from jax import lax
from jax.sharding import Mesh
from jax.sharding import PartitionSpec as P

COL = ("col_0", "col_1", "col_2")
DP_COL = ("dp", "col_0", "col_1", "col_2")


root_term = 0.7978845608028654
cubic_term = 0.044715


def side_by_side(arrays, axis, dim, along):
    widths = [a.shape[along] for a in arrays]
    both = jnp.concatenate(arrays, axis=along)
    result = lax.all_gather(both, axis, axis=dim, tiled=True)
    return tuple(jnp.split(result, [sum(widths[:k]) for k in range(1, len(widths))], axis=along))


def cut_along(shard, dim, length):
    before, after = (shard.shape[:dim], shard.shape[dim + 1 :])
    return jnp.moveaxis(shard.reshape(*before, length, -1, *after), dim, 0)


def sum_by_chip(shard, chips, core, dim):
    sizes = (lax.axis_size(chips), lax.axis_size(core))
    blocks = cut_along(shard, dim, sizes[0] * sizes[1])
    inside = blocks.shape[1:]
    blocks = blocks.reshape(*sizes, *inside).swapaxes(0, 1).reshape(-1, *inside)
    blocks = lax.psum_scatter(blocks, core, scatter_dimension=0, tiled=True)
    return lax.psum_scatter(blocks, chips, scatter_dimension=0, tiled=True)[0]


def sent_to_all(shard, axis):
    length = lax.axis_size(axis)
    return lax.all_to_all(
        jnp.broadcast_to(shard[None], (length, *shard.shape)), axis, 0, 0, tiled=True
    )


def of_everyone(shard, axis):
    return sent_to_all(shard, axis).sum(axis=0)


def gelu_pair(values):
    inside = root_term * (values + cubic_term * values * values * values)
    tangent = jnp.tanh(inside)
    activated = 0.5 * values * (1.0 + tangent)
    derivative = 0.5 * (1.0 + tangent) + 0.5 * values * (1.0 - tangent * tangent) * root_term * (
        1.0 + 3.0 * cubic_term * values * values
    )
    return (activated, derivative)


def unpack_stash(stash_codes, stash_scales):
    blocks = stash_scales.shape[1]
    block_width = stash_codes.shape[1] // blocks
    levels = (
        (2 * stash_codes - 3).astype(jnp.float32).reshape(stash_codes.shape[0], blocks, block_width)
    )
    scaled = levels * stash_scales.astype(jnp.float32)[:, :, None] / 16.0
    return scaled.reshape(stash_codes.shape).astype(jnp.bfloat16)


def per_device(stash_codes, stash_scales, pad_mask, cotangent, w_gate, w_up, w_out):
    stashed = unpack_stash(stash_codes, stash_scales)
    live_grad = (cotangent.astype(jnp.float32) * pad_mask.astype(jnp.float32)[:, None]).astype(
        jnp.bfloat16
    )
    stash_all, grad_all = side_by_side((stashed, live_grad), COL, 0, 1)
    ff_local = w_gate.shape[1]
    joined = lax.psum_scatter(
        jnp.concatenate(
            [
                jnp.dot(stash_all, w_gate, preferred_element_type=jnp.float32),
                jnp.dot(stash_all, w_up, preferred_element_type=jnp.float32),
                jnp.dot(grad_all, w_out, preferred_element_type=jnp.float32),
            ],
            axis=1,
        ),
        "row",
        scatter_dimension=0,
        tiled=True,
    )
    gate_pre = joined[:, :ff_local]
    up_part = joined[:, ff_local : 2 * ff_local]
    back_grad = joined[:, 2 * ff_local :]
    activated, derivative = gelu_pair(gate_pre)
    hidden = (activated * up_part).astype(jnp.bfloat16)
    gate_grad = (back_grad * up_part * derivative).astype(jnp.bfloat16)
    up_grad = (back_grad * activated).astype(jnp.bfloat16)
    local_stack = jnp.concatenate([gate_grad, up_grad, hidden], axis=1)
    stacked = lax.all_gather(local_stack, "row", axis=0, tiled=True)
    transposed = (((1,), (1,)), ((), ()))
    gate_rows = stacked[:, :ff_local]
    up_rows = stacked[:, ff_local : 2 * ff_local]
    input_grad = sum_by_chip(
        lax.dot_general(gate_rows, w_gate, transposed, preferred_element_type=jnp.float32)
        + lax.dot_general(up_rows, w_up, transposed, preferred_element_type=jnp.float32),
        ("col_0", "col_1"),
        "col_2",
        0,
    )
    contract = (((0,), (0,)), ((), ()))
    inputs_part = lax.dot_general(
        stash_all, stacked[:, : 2 * ff_local], contract, preferred_element_type=jnp.float32
    )
    second = lax.dot_general(
        grad_all, stacked[:, 2 * ff_local :], contract, preferred_element_type=jnp.float32
    )
    summed = of_everyone(jnp.concatenate([inputs_part, second], axis=1), "dp")
    return (
        input_grad,
        summed[:, :ff_local],
        summed[:, ff_local : 2 * ff_local],
        summed[:, 2 * ff_local :],
    )


def solution(mesh):
    finer = Mesh(
        mesh.devices.reshape(mesh.shape["dp"], mesh.shape["row"], 2, 4, 2),
        ("dp", "row", "col_0", "col_1", "col_2"),
    )
    in_specs = (
        P(DP_COL, "row"),
        P(DP_COL, "row"),
        P(DP_COL),
        P(DP_COL, "row"),
        P("row", COL),
        P("row", COL),
        P("row", COL),
    )
    out_specs = (P(DP_COL, "row"), P("row", COL), P("row", COL), P("row", COL))
    return jax.shard_map(
        per_device, mesh=finer, in_specs=in_specs, out_specs=out_specs, check_vma=False
    )
```

profile of v0, /device:TPU:0, one launch (start us, length us, event | category | flops | bytes accessed | tf_op | source)
XLA Modules:
  0.0 590.7 jit_solution(5459512023354800556)
XLA Ops:
  7.2 0.0 copy-start
  7.2 0.0 copy-start.3
  7.2 0.0 all-gather.3.cloned.1.call-start
  7.2 0.8 convert_element_type.31
  8.0 0.7 convert_element_type.28
  8.7 0.1 copy.14
  8.8 0.2 mul.85
  9.0 1.3 fusion.23
  10.4 0.8 pad_maximum_fusion.3
  11.2 0.0 all-gather.3.cloned.1.call-update
  11.2 0.0 reduce-scatter.4.cloned.1.call-start
  11.3 54.7 %all-gather.3.cloned.1.call-done = bf16[2048,2048]{1,0:T(8,128)(2,1)} async-done(((bf16[128,2048]{1,0:T(8,128)(2,1)}), bf16[2048,2048]{1,0:T(8,128)(2,1)}) %all-gather.3.cloned.1.call-update) | async-done | bytes 8388624 | tf_op jit(solution)/shard_map/all_gather | solution.py:18
  66.0 0.0 copy-done.3
  66.0 0.0 copy-start.4
  66.0 0.0 copy-start.5
  66.0 4.9 fusion.7
  70.9 0.0 copy-done.4
  70.9 0.0 copy-done.5
  70.9 3.1 fusion.4
  74.0 0.0 copy-done
  74.0 3.0 fusion.9
  77.1 5.9 pad_maximum_fusion
  83.0 0.0 reduce-scatter.4.cloned.1.call-update
  83.0 0.0 all-gather.5.cloned.1.call-start
  83.0 140.9 %reduce-scatter.4.cloned.1.call-done = f32[512,1920]{0,1:T(8,128)} async-done(((f32[2048,1920]{0,1:T(8,128)}), f32[512,1920]{0,1:T(8,128)}) %reduce-scatter.4.cloned.1.call-update) | async-done | bytes 3932176 | tf_op jit(solution)/shard_map/reduce_scatter | solution.py:74
  223.9 3.2 fusion.21
  227.1 1.4 pad_maximum_fusion.2
  228.5 0.0 all-gather.5.cloned.1.call-update
  228.5 0.2 reduce-scatter.6.cloned.1.call-start
  228.8 78.3 %all-gather.5.cloned.1.call-done = bf16[2048,1920]{0,1:T(8,128)(2,1)} async-done(((bf16[512,1920]{0,1:T(8,128)(2,1)}), bf16[2048,1920]{0,1:T(8,128)(2,1)}) %all-gather.5.cloned.1.call-update) | async-done | bytes 7864336 | tf_op jit(solution)/shard_map/all_gather | solution.py:95
  307.1 0.0 copy-start.2
  307.1 5.4 fusion.13
  312.6 0.0 copy-done.2
  312.6 3.6 convolution_add_fusion
  316.2 4.0 copy.15
  320.2 0.0 reduce-scatter.6.cloned.1.call-update
  320.2 0.3 reduce-scatter.8.cloned.1.call-start
  320.5 8.0 %fusion.2 = f32[1024,640]{1,0:T(8,128)} fusion(bf16[2048,2048]{1,0:T(8,128)(2,1)} %all-gather.3.cloned.1.call-done, bf16[2048,1920]{0,1:T(8,128)(2,1)} %all-gather.5.cloned.1.call-done), kind=kOutput, calls=%fused_computation.5 | convolution fusion | flops 2684354560 | bytes 9437184 | tf_op jit(solution)/shard_map/dot_general | solution.py:110
  328.5 11.2 %fusion = f32[1024,1280]{1,0:T(8,128)} fusion(bf16[2048,1920]{0,1:T(8,128)(2,1)} %all-gather.5.cloned.1.call-done, bf16[2048,2048]{1,0:T(8,128)(2,1)} %all-gather.3.cloned.1.call-done), kind=kOutput, calls=%fused_computation.2 | convolution fusion | flops 5368709120 | bytes 14680064 | tf_op jit(solution)/shard_map/dot_general | solution.py:107
  339.7 0.7 reduce-scatter.6.cloned.1.call-done
  340.4 0.0 reduce-scatter.8.cloned.1.call-update
  340.5 7.0 %pad_maximum_fusion.1 = f32[1024,1920]{1,0:T(8,128)} fusion(f32[1024,640]{1,0:T(8,128)} %fusion.2, f32[1024,1280]{1,0:T(8,128)} %fusion), kind=kLoop, calls=%fused_computation.1 | loop fusion | flops 1966080 | bytes 15728640 | tf_op jit(solution)/shard_map/concatenate | solution.py:113
  347.4 9.8 %broadcast_in_dim.2 = f32[2,1024,1920]{2,1,0:T(8,128)} broadcast(f32[1024,1920]{1,0:T(8,128)} %pad_maximum_fusion.1), dimensions={1,2} | broadcast | bytes 23592960 | tf_op jit(solution)/shard_map/broadcast_in_dim | solution.py:39
  357.3 209.7 %all_to_all.5 = f32[2,1024,1920]{2,1,0:T(8,128)} all-to-all(f32[2,1024,1920]{2,1,0:T(8,128)} %broadcast_in_dim.2), channel_id=1, replica_groups=mesh['dp'=2,'row'=4,'col_0'=2,'col_1'=4,'col_2'=2] {'dp'}, dimensions={0} | all-to-all | bytes 31457280 | tf_op jit(solution)/shard_map/all_to_all | solution.py:38
  566.9 10.4 %reduce_sum.9 = f32[1024,1920]{1,0:T(8,128)} reduce(f32[2,1024,1920]{2,1,0:T(8,128)} %all_to_all.5, f32[]{:T(128)} %constant.19.clone.1), dimensions={0}, to_apply=%region_3.0 | reduce | flops 1966080 | bytes 23592964 | tf_op jit(solution)/shard_map/reduce_sum | solution.py:44
  577.4 0.0 copy-start.1
  577.4 6.8 %fusion.24 = (f32[1024,640]{1,0:T(8,128)}, f32[1024,640]{1,0:T(8,128)}, f32[1024,640]{1,0:T(8,128)}) fusion(f32[1024,1920]{1,0:T(8,128)} %reduce_sum.9), kind=kLoop, calls=%fused_computation.36 | loop fusion | bytes 15728640 | tf_op jit(solution)/shard_map/slice | solution.py:118
  584.2 0.0 copy-done.1
  (1 shorter events, 0.0 us)
Async XLA Ops:
  7.2 66.9 %copy-start = (bf16[1024,640]{1,0:T(8,128)(2,1)S(1)}, bf16[1024,640]{1,0:T(8,128)(2,1)}, u32[]{:S(2)}) copy-start(bf16[1024,640]{1,0:T(8,128)(2,1)} %param.11) | copy-start | bytes 3932164
  7.2 58.8 %copy-start.3 = (bf16[1024,640]{1,0:T(8,128)(2,1)S(1)}, bf16[1024,640]{1,0:T(8,128)(2,1)}, u32[]{:S(2)}) copy-start(bf16[1024,640]{1,0:T(8,128)(2,1)} %param.12) | copy-start | bytes 3932164
  7.2 58.8 %all-gather.3.cloned.1.call-start = ((), (), s32[]{:S(2)}) async-start(), calls=%async_computation.4 | async-start | bytes 8912896 | tf_op jit(solution)/shard_map/all_gather | solution.py:18
  11.2 212.7 %reduce-scatter.4.cloned.1.call-start = ((), (), s32[]{:S(2)}) async-start(), calls=%async_computation.5 | async-start | bytes 19660800 | tf_op jit(solution)/shard_map/reduce_scatter | solution.py:74
  66.0 5.0 copy-start.4
  66.0 5.0 copy-start.5
  83.0 224.1 %all-gather.5.cloned.1.call-start = ((), (), s32[]{:S(2)}) async-start(), calls=%async_computation.6 | async-start | bytes 9830400 | tf_op jit(solution)/shard_map/all_gather | solution.py:95
  228.5 111.9 %reduce-scatter.6.cloned.1.call-start = ((), (), s32[]{:S(2)}) async-start(), calls=%async_computation.7 | async-start | bytes 12582912 | tf_op jit(solution)/shard_map/reduce_scatter | solution.py:32
  307.1 5.4 copy-start.2
  320.2 263.9 %reduce-scatter.8.cloned.1.call-start = ((), (), s32[]{:S(2)}) async-start(), calls=%async_computation.8 | async-start | bytes 4718592 | tf_op jit(solution)/shard_map/reduce_scatter | solution.py:33
  577.4 6.8 %copy-start.1 = (bf16[1024,640]{1,0:T(8,128)(2,1)S(1)}, bf16[1024,640]{1,0:T(8,128)(2,1)}, u32[]{:S(2)}) copy-start(bf16[1024,640]{1,0:T(8,128)(2,1)} %param.11) | copy-start | bytes 3932164
Sparse Core Ops, SparseCore 0:
  11.4 54.5 all-gather.2
  83.1 140.7 reduce-scatter.3
  228.7 78.4 all-gather.4
  320.4 20.0 reduce-scatter.5
  343.3 54.6 reduce-scatter.7
where the time goes:
time: 592 us; the launch traced here: 591 us
  waiting for transfers between devices  275 us (46%)
  blocking collectives  210 us (35%)
  matrix products  39.3 us (7%)
  other arithmetic  31.5 us (5%)
  local copies, waits for them, and re-layouts  21 us (4%)
  between operations  13.9 us (2%)
    all_to_all x1, blocking collectives, sent_to_all(): lax.all_to_all(jnp.broadcast_to(shard[None], (length, *shard.shape)), axi...  210 us
    reduce_scatter x1, waiting for transfers between devices, per_device(): lax.psum_scatter(jnp.concatenate([jnp.dot(stash_all, w_gate, preferred_el...  141 us
    all_gather x1, waiting for transfers between devices, per_device(): stacked = lax.all_gather(local_stack, 'row', axis=0, tiled=True)  78.3 us
    all_gather x1, waiting for transfers between devices, side_by_side(): result = lax.all_gather(both, axis, axis=dim, tiled=True)  54.7 us
  transfers between devices with their start and end apart: 5, of which 4 were waited for; matrix products, arithmetic and copies ran while one was open for 9% of the time, Pallas kernels for 0%

commit v1 on v0

v1 whole, which is shorter than its diff:
```python
import functools

import jax
import jax.numpy as jnp
from jax import lax
from jax.experimental import pallas as pl
from jax.experimental.pallas import tpu as pltpu
from jax.sharding import PartitionSpec as P

MESH = pl.DeviceIdType.MESH
ROOT = 0.7978845608028654
CUBIC = 0.044715
W = 128
FOOT = 16
F32 = jnp.float32
BF16 = jnp.bfloat16


def gelu_pair(values):
    inside = ROOT * (values + CUBIC * values * values * values)
    tangent = jnp.tanh(inside)
    activated = 0.5 * values * (1.0 + tangent)
    derivative = 0.5 * (1.0 + tangent) + 0.5 * values * (1.0 - tangent * tangent) * ROOT * (
        1.0 + 3.0 * CUBIC * values * values
    )
    return activated, derivative


def coded(part):
    most = jnp.maximum(jnp.max(jnp.abs(part), axis=0, keepdims=True), 1e-30)
    power = jnp.floor(jnp.log(most) * 1.4426950408889634) + 1.0
    units = jnp.round(part * jnp.exp2(15.0 - power))
    units = jnp.clip(units, -32767.0, 32767.0).astype(jnp.int32).astype(jnp.int16)
    foot = jnp.broadcast_to(power, (FOOT, part.shape[1])).astype(jnp.int32).astype(jnp.int16)
    return units, foot


def store_coded(tile, lanes, part):
    rows = part.shape[0]
    units, foot = coded(part)
    tile[pl.ds(0, rows), lanes] = units
    tile[pl.ds(rows, FOOT), lanes] = foot


def decoded(tile, rows, lanes):
    power = tile[pl.ds(rows, FOOT), lanes].astype(jnp.int32).astype(F32)[0:1]
    units = tile[pl.ds(0, rows), lanes].astype(jnp.int32).astype(F32)
    return units * jnp.exp2(power - 15.0)


def kernel(
    dims,
    codes, scales, mask, cot, wg, wu, wo,
    dx_out, g_out, u_out, o_out,
    sl, wc, pb, r1, r2, guh, dx, dws, dwr, stage, dxs, dxr, dfr,
    w_sem, ag_s, ag_r, rs1_s, rs1_r, rs2_s, rs2_r, a1_s, a1_r, a2_s, a2_r,
    dp_s, dp_r, out_sem, dxc_s, dxc_r, dx_s, dx_r,
):
    tb, dl, chunks = dims
    blk = 4 * tb
    half = 2 * tb
    x = lax.axis_index("row")
    col = lax.axis_index("col")
    dp = lax.axis_index("dp")
    core = lax.rem(col, 2)
    y = lax.rem(col // 2, 4)
    z = col // 8
    right, left, opp = lax.rem(x + 1, 4), lax.rem(x + 3, 4), lax.rem(x + 2, 4)

    def at_col(dz, dy, dc):
        zz = (1 - z) if dz else z
        cc = (1 - core) if dc else core
        return {"col": (zz * 4 + lax.rem(y + dy, 4)) * 2 + cc}

    to_right, to_left, to_dp = {"row": right}, {"row": left}, {"dp": 1 - dp}
    STEP = (0, 3, 1, 2)
    others = [(b, zr) for b in range(4) for zr in range(2) if (b, zr) != (0, 0)]

    barrier = pltpu.get_barrier_semaphore()
    peers = [to_right, to_left, to_dp, at_col(0, 0, 1)]
    peers += [at_col(zr, STEP[b], 0) for b, zr in others]
    for peer in peers:
        pl.semaphore_signal(barrier, inc=1, device_id=peer, device_id_type=MESH)

    def weight_copy(j, m, src):
        return pltpu.make_async_copy(
            src.at[:, pl.ds(j * W, W)], wc.at[j, :, pl.ds(m * W, W)], w_sem.at[j, m]
        )

    for j in range(chunks):
        for m, src in enumerate((wg, wu, wo)):
            weight_copy(j, m, src).start()

    for k in range(dl // 128):
        lanes = pl.ds(k * 128, 128)
        level = (2 * codes[:, lanes] - 3) * scales[:, k : k + 1]
        sl[pl.ds(0, tb), lanes] = (level.astype(F32) * 0.0625).astype(BF16)
        live = cot[:, lanes].astype(F32) * mask[...].astype(F32)
        sl[pl.ds(0, tb), pl.ds(dl + k * 128, 128)] = live.astype(BF16)

    pl.semaphore_wait(barrier, len(peers))

    def remote(src, dst, s_sem, r_sem, device):
        return pltpu.make_async_remote_copy(
            src_ref=src, dst_ref=dst, send_sem=s_sem, recv_sem=r_sem,
            device_id=device, device_id_type=MESH,
        )

    def slot(b, zr, cr):
        return (b * 4 + zr * 2 + cr) * tb

    def rows(start, count):
        return sl.at[pl.ds(start, count)]

    started = []

    def gather(kind, src, dst, count, device):
        copy = remote(rows(src, count), rows(dst, count), ag_s.at[kind], ag_r.at[kind], device)
        copy.start()
        started.append(copy)

    def arrived(kind, dst, count):
        remote(
            rows(dst, count), rows(dst, count), ag_s.at[kind], ag_r.at[kind], at_col(0, 0, 1)
        ).wait_recv()

    def to_core(kind, b, zr):
        gather(9 + kind, slot(b, zr, 0), slot(b, zr, 1), tb, at_col(0, 0, 1))

    up, down = at_col(0, 1, 0), at_col(0, 3, 0)
    part = tb // 2
    gather(0, slot(0, 0, 0), slot(0, 1, 0), tb, at_col(1, 0, 0))
    gather(1, slot(0, 0, 0), slot(1, 0, 0), tb, up)
    gather(2, slot(0, 0, 0), slot(2, 0, 0), tb, down)
    to_core(0, 0, 0)
    for j in range(chunks):
        for m, src in enumerate((wg, wu, wo)):
            weight_copy(j, m, src).wait()

    def forward(j, b):
        into = pb.at[lax.rem(j, 3)]
        for h in range(2):
            where = pl.ds(pl.multiple_of(b * blk + h * half, half), half)
            tile = into.at[b, h]
            both = jnp.dot(
                sl[where, pl.ds(0, dl)], wc[j, :, pl.ds(0, 2 * W)], preferred_element_type=F32
            )
            store_coded(tile, pl.ds(0, 2 * W), both)
            back = jnp.dot(
                sl[where, pl.ds(dl, dl)], wc[j, :, pl.ds(2 * W, W)], preferred_element_type=F32
            )
            store_coded(tile, pl.ds(2 * W, W), back)

    def rs1(j, way):
        into = pb.at[lax.rem(j, 3)]
        return remote(
            into.at[opp, way], r1.at[j, way], rs1_s.at[j, way], rs1_r.at[j, way],
            (to_right, to_left)[way],
        )

    def rs2(j, way):
        into = pb.at[lax.rem(j, 3)]
        return remote(
            into.at[(right, left)[way]], r2.at[j, way], rs2_s.at[j, way], rs2_r.at[j, way],
            (to_right, to_left)[way],
        )

    def block_rows(j, b):
        return guh.at[j, pl.ds(pl.multiple_of(b * blk, blk), blk)]

    def half_rows(j, b, h):
        return guh.at[j, pl.ds(pl.multiple_of(b * blk + h * half, half), half)]

    def a1(j, way):
        return remote(
            block_rows(j, x), block_rows(j, x), a1_s.at[j, way], a1_r.at[j, way],
            (to_right, to_left)[way],
        )

    def a1_arrival(j, way):
        from_block = (left, right)[way]
        return remote(
            block_rows(j, from_block), block_rows(j, from_block), a1_s.at[j, way],
            a1_r.at[j, way], (to_right, to_left)[way],
        )

    def a2(j, way):
        b = (left, right)[way]
        return remote(
            half_rows(j, b, way), half_rows(j, b, way), a2_s.at[j, way], a2_r.at[j, way],
            (to_right, to_left)[way],
        )

    def a2_arrival(j, way):
        return remote(
            half_rows(j, opp, way), half_rows(j, opp, way), a2_s.at[j, way], a2_r.at[j, way],
            (to_right, to_left)[way],
        )

    def send_rs1(j):
        for way in range(2):
            rs1(j, way).start()

    def stage_f(j):
        def body(b, carry):
            forward(j, b)
            return carry

        lax.fori_loop(0, 4, body, 0)
        send_rs1(j)

    def stage_r(j):
        into = pb.at[lax.rem(j, 3)]
        for way in range(2):
            rs1(j, way).wait_recv()
            tile = into.at[(right, left)[way], way]
            for m in range(3):
                lanes = pl.ds(m * W, W)
                total = decoded(tile, half, lanes) + decoded(r1.at[j, way], half, lanes)
                store_coded(tile, lanes, total)
            rs2(j, way).start()

    def stage_a(j):
        into = pb.at[lax.rem(j, 3)]
        for way in range(2):
            rs2(j, way).wait_recv()
        for h in range(2):
            powers = []
            for m in range(3):
                lanes = pl.ds(m * W, W)
                powers.append(
                    [
                        jnp.exp2(
                            t[pl.ds(half, FOOT), lanes].astype(jnp.int32).astype(F32)[0:1] - 15.0
                        )
                        for t in (into.at[x, h], r2.at[j, 0, h], r2.at[j, 1, h])
                    ]
                )

            def body(k, carry, h=h, powers=powers):
                some = pl.ds(pl.multiple_of(k * 64, 64), 64)
                sums = []
                for m in range(3):
                    lanes = pl.ds(m * W, W)
                    total = None
                    for t, power in zip((into.at[x, h], r2.at[j, 0, h], r2.at[j, 1, h]), powers[m]):
                        term = t[some, lanes].astype(jnp.int32).astype(F32) * power
                        total = term if total is None else total + term
                    sums.append(total)
                gate, up_part, back = sums
                activated, derivative = gelu_pair(gate)
                to = pl.ds(pl.multiple_of(x * blk + h * half + k * 64, 64), 64)
                guh[j, to, pl.ds(0, W)] = (back * up_part * derivative).astype(BF16)
                guh[j, to, pl.ds(W, W)] = (back * activated).astype(BF16)
                guh[j, to, pl.ds(2 * W, W)] = (activated * up_part).astype(BF16)
                return carry

            lax.fori_loop(0, half // 64, body, 0)
        for way in range(2):
            a1(j, way).start()
        for way in range(2):
            rs1(j, way).wait_send()
            rs2(j, way).wait_send()

    def stage_w(j):
        for way in range(2):
            a1_arrival(j, way).wait_recv()
            a2(j, way).start()

    def dp_copy(j):
        return remote(dws.at[j], dwr.at[j], dp_s.at[j], dp_r.at[j], to_dp)

    def stage_dx(j):
        for way in range(2):
            a2_arrival(j, way).wait_recv()

        def body(k, carry):
            where = pl.ds(pl.multiple_of(k * half, half), half)
            more = lax.dot_general(
                guh[j, where, pl.ds(0, 2 * W)], wc[j, :, pl.ds(0, 2 * W)],
                (((1,), (1,)), ((), ())), preferred_element_type=F32,
            )
            dx[where, :] = dx[where, :] + more
            return carry

        lax.fori_loop(0, 8, body, 0)

    def stage_dw(j):
        def body(k, carry):
            where = pl.ds(pl.multiple_of(k * 256, 256), 256)
            some = lax.dot_general(
                sl[:, where], guh[j, :, pl.ds(0, 2 * W)],
                (((0,), (0,)), ((), ())), preferred_element_type=F32,
            )
            dws[j, where, pl.ds(0, 2 * W)] = some.astype(BF16)
            last = lax.dot_general(
                sl[:, pl.ds(pl.multiple_of(dl + k * 256, 256), 256)], guh[j, :, pl.ds(2 * W, W)],
                (((0,), (0,)), ((), ())), preferred_element_type=F32,
            )
            dws[j, where, pl.ds(2 * W, W)] = last.astype(BF16)
            return carry

        lax.fori_loop(0, dl // 256, body, 0)
        dp_copy(j).start()

    def out_copy(j, m):
        return pltpu.make_async_copy(
            stage.at[lax.rem(j, 2), m],
            (g_out, u_out, o_out)[m].at[:, pl.ds(pl.multiple_of(j * W, W), W)],
            out_sem.at[j, m],
        )

    def stage_e(j):
        dp_copy(j).wait()

        @pl.when(j >= 2)
        def _():
            for m in range(3):
                out_copy(j - 2, m).wait()

        def body(k, carry):
            where = pl.ds(pl.multiple_of(k * 128, 128), 128)
            for m in range(3):
                lanes = pl.ds(m * W, W)
                stage[lax.rem(j, 2), m, where, :] = dws[j, where, lanes].astype(F32) + dwr[
                    j, where, lanes
                ].astype(F32)
            return carry

        lax.fori_loop(0, dl // 128, body, 0)
        for m in range(3):
            out_copy(j, m).start()

    arrived(0, slot(0, 1, 0), tb)
    gather(3, slot(0, 1, 0), slot(1, 1, 0), tb, up)
    gather(4, slot(0, 1, 0), slot(2, 1, 0), tb, down)
    to_core(1, 0, 1)
    arrived(1, slot(1, 0, 0), tb)
    gather(5, slot(1, 0, 0), slot(3, 0, 0), part, up)
    to_core(2, 1, 0)
    arrived(2, slot(2, 0, 0), tb)
    gather(6, slot(2, 0, 0) + part, slot(3, 0, 0) + part, part, down)
    to_core(3, 2, 0)
    arrived(9, slot(0, 0, 1), tb)
    arrived(10, slot(0, 1, 1), tb)
    forward(0, 0)
    arrived(3, slot(1, 1, 0), tb)
    gather(7, slot(1, 1, 0), slot(3, 1, 0), part, up)
    to_core(4, 1, 1)
    arrived(4, slot(2, 1, 0), tb)
    gather(8, slot(2, 1, 0) + part, slot(3, 1, 0) + part, part, down)
    to_core(5, 2, 1)
    arrived(11, slot(1, 0, 1), tb)
    arrived(13, slot(1, 1, 1), tb)
    forward(0, 1)
    arrived(12, slot(2, 0, 1), tb)
    arrived(14, slot(2, 1, 1), tb)
    forward(0, 2)
    arrived(5, slot(3, 0, 0), part)
    arrived(6, slot(3, 0, 0) + part, part)
    to_core(6, 3, 0)
    arrived(7, slot(3, 1, 0), part)
    arrived(8, slot(3, 1, 0) + part, part)
    to_core(7, 3, 1)
    arrived(15, slot(3, 0, 1), tb)
    arrived(16, slot(3, 1, 1), tb)
    forward(0, 3)
    send_rs1(0)
    dx[...] = jnp.zeros_like(dx)

    def step(t, carry):
        def at(lag, fn, least=0):
            @pl.when(jnp.logical_and(t - lag >= least, t - lag < chunks))
            def _():
                fn(t - lag)

        at(0, stage_f, 1)
        at(1, stage_r)
        at(2, stage_a)
        at(3, stage_w)
        at(4, stage_dx)
        at(4, stage_dw)
        at(6, stage_e)
        return carry

    lax.fori_loop(0, chunks + 4, step, 0)

    core_copy = remote(dxs, dxr, dxc_s.at[0], dxc_r.at[0], at_col(0, 0, 1))
    for i in range(8):
        dxs[i] = dx[pl.ds((2 * i + 1) * tb, tb), :].astype(BF16)
    core_copy.start()
    for j in range(chunks - 2, chunks - 1):
        stage_e(j)
    core_copy.wait()

    def chip_copy(i):
        b, zr = i // 2, i % 2
        return remote(
            dxs.at[i], dfr.at[i], dx_s.at[i], dx_r.at[i], at_col(zr, STEP[b], 0)
        )

    for i in range(1, 8):
        total = dx[pl.ds(2 * i * tb, tb), :] + dxr[i].astype(F32)
        dxs[i] = total.astype(BF16)
        chip_copy(i).start()
    stage_e(chunks - 1)
    total = dx[pl.ds(0, tb), :] + dxr[0].astype(F32)
    for i in range(1, 8):
        chip_copy(i).wait()
        total = total + dfr[i].astype(F32)
    dx_out[...] = total

    for copy in started:
        copy.wait_send()
    for j in range(chunks):
        for way in range(2):
            a1(j, way).wait_send()
            a2(j, way).wait_send()
    for j in range(chunks - 2, chunks):
        for m in range(3):
            out_copy(j, m).wait()


def per_device(codes, scales, mask, cot, wg, wu, wo):
    tb, dl = codes.shape
    fl = wg.shape[1]
    chunks = fl // W
    dims = (tb, dl, chunks)
    tile = 2 * tb + FOOT
    vmem = pl.BlockSpec(memory_space=pltpu.VMEM)
    hbm = pl.BlockSpec(memory_space=pl.ANY)
    dma = pltpu.SemaphoreType.DMA
    weight = jax.ShapeDtypeStruct((dl, fl), F32)
    return pl.pallas_call(
        functools.partial(kernel, dims),
        out_shape=(jax.ShapeDtypeStruct((tb, dl), F32), weight, weight, weight),
        in_specs=[vmem] * 4 + [hbm] * 3,
        out_specs=(vmem, hbm, hbm, hbm),
        scratch_shapes=[
            pltpu.VMEM((16 * tb, 2 * dl), BF16),
            pltpu.VMEM((chunks, dl, 3 * W), BF16),
            pltpu.VMEM((3, 4, 2, tile, 3 * W), jnp.int16),
            pltpu.VMEM((chunks, 2, tile, 3 * W), jnp.int16),
            pltpu.VMEM((chunks, 2, 2, tile, 3 * W), jnp.int16),
            pltpu.VMEM((chunks, 16 * tb, 3 * W), BF16),
            pltpu.VMEM((16 * tb, dl), F32),
            pltpu.VMEM((chunks, dl, 3 * W), BF16),
            pltpu.VMEM((chunks, dl, 3 * W), BF16),
            pltpu.VMEM((2, 3, dl, W), F32),
            pltpu.VMEM((8, tb, dl), BF16),
            pltpu.VMEM((8, tb, dl), BF16),
            pltpu.VMEM((8, tb, dl), BF16),
            dma((chunks, 3)),
            dma((17,)), dma((17,)),
            dma((chunks, 2)), dma((chunks, 2)),
            dma((chunks, 2)), dma((chunks, 2)),
            dma((chunks, 2)), dma((chunks, 2)),
            dma((chunks, 2)), dma((chunks, 2)),
            dma((chunks,)), dma((chunks,)),
            dma((chunks, 3)),
            dma((1,)), dma((1,)),
            dma((8,)), dma((8,)),
        ],
        compiler_params=pltpu.CompilerParams(
            collective_id=0, has_side_effects=True, vmem_limit_bytes=67043328
        ),
        name="ffn_backward",
    )(codes, scales, mask[:, None], cot, wg, wu, wo)


def solution(mesh):
    tokens = P(("dp", "col"), "row")
    weights = P("row", "col")
    return jax.shard_map(
        per_device,
        mesh=mesh,
        in_specs=(tokens, tokens, P(("dp", "col")), tokens, weights, weights, weights),
        out_specs=(tokens, weights, weights, weights),
        check_vma=False,
    )
```

time: 592 us -> 260 us (0.44)
  waiting for transfers between devices: 275 us -> 0 us
  Pallas kernels: 0 us -> 245 us
  blocking collectives: 210 us -> 0 us
  matrix products: 39.3 us -> 0 us
  other arithmetic: 31.5 us -> 0 us
  between operations: 13.9 us -> 0.64 us
  local copies, waits for them, and re-layouts: 21 us -> 12.4 us
    pallas_call x0 -> x1, Pallas kernels: none -> 245 us  [per_device(): pl.pallas_call(functools.partial(kernel, dims), out_shape=(jax.ShapeDtype...]
    all_to_all x1 -> x0, blocking collectives: 210 us -> none  [sent_to_all(): lax.all_to_all(jnp.broadcast_to(shard[None], (length, *shard.shape)), axi...]
    reduce_scatter x3 -> x0, waiting for transfers between devices: 142 us -> none  [the longest x1 141 us: per_device(): lax.psum_scatter(jnp.concatenate([jnp.dot(stash_all, w_gate, preferred_el...]
    all_gather x2 -> x0, waiting for transfers between devices: 133 us -> none  [the longest x1 78.3 us: per_device(): stacked = lax.all_gather(local_stack, 'row', axis=0, tiled=True)]
    dot_general x7 -> x0, matrix products: 39.3 us -> none  [the longest x1 11.2 us: per_device(): lax.dot_general(stash_all, stacked[:, :2 * ff_local], contract, preferred...]
    concatenate x4 -> x0, other arithmetic: 15.1 us -> none  [the longest x1 6.99 us: per_device(): summed = of_everyone(jnp.concatenate([inputs_part, second], axis=1), 'dp')]
    unnamed x12 -> x9, local copies, waits for them, and re-layouts: 0.03 us -> 11 us
    reduce_sum x1 -> x0, other arithmetic: 10.4 us -> none  [of_everyone(): return sent_to_all(shard, axis).sum(axis=0)]
  transfers between devices with their start and end apart: 5 -> 0, of which waited for: 4 -> 0; matrix products, arithmetic and copies ran while one was open for 9% -> 0% of each run, Pallas kernels for 0% -> 0%
where the time goes in v1:
time: 260 us; the launch traced here: 258 us
  Pallas kernels  245 us (94%)
  local copies, waits for them, and re-layouts  12.4 us (5%)
    pallas_call x1, Pallas kernels, per_device(): pl.pallas_call(functools.partial(kernel, dims), out_shape=(jax.ShapeDtype...  245 us
    unnamed x9, local copies, waits for them, and re-layouts  11 us

profile of v1, /device:TPU:0, one launch (start us, length us, event | category | flops | bytes accessed | tf_op | source)
XLA Modules:
  0.0 258.0 jit_solution(9394124155693499607)
XLA Ops:
  0.6 1.4 copy.11.scales
  2.0 1.4 copy.12.mask
  3.4 244.9 %ffn_backward.1 = (f32[128,1024]{1,0:T(8,128)}, f32[1024,640]{1,0:T(8,128)}, f32[1024,640]{1,0:T(8,128)}, f32[1024,640]{1,0:T(8,128)}) custom-call(s32[128,1024]{1,0:T(8,128)} %codes.1, s32[128,8]{1,0:T(8,128)} %copy.11.scales, s32[128,1]{1,0:T(8,128)} %copy.12.mask, bf16[128,1024]{1,0:T(8,128)(2,1)} %cot.1, bf16[1024,640]{1,0:T(8,128)(2,1)} %wg.1, ...), custom_call_target="tpu_custom_call" | custom-call | tf_op jit(solution)/shard_map/ffn_backward/pallas_call | solution.py:434
  248.4 1.9 copy.17
  250.2 0.0 copy-start.1
  250.2 3.5 %copy.18 = f32[1024,640]{1,0:T(8,128)} copy(f32[1024,640]{1,0:T(8,128)} %get-tuple-element.9) | data formatting | bytes 5242880
  253.8 0.0 copy-done.1
  253.8 0.0 copy-start
  253.8 1.5 copy.19
  255.3 1.2 copy-done
  256.5 1.5 copy.20
Async XLA Ops:
  250.2 3.6 %copy-start.1 = (f32[1024,640]{1,0:T(8,128)S(1)}, f32[1024,640]{1,0:T(8,128)}, u32[]{:S(2)}) copy-start(f32[1024,640]{1,0:T(8,128)} %get-tuple-element.10) | copy-start | bytes 7864324
  253.8 2.7 %copy-start = (f32[1024,640]{1,0:T(8,128)S(1)}, f32[1024,640]{1,0:T(8,128)}, u32[]{:S(2)}) copy-start(f32[1024,640]{1,0:T(8,128)} %get-tuple-element.11) | copy-start | bytes 7864324

commit v2 on v1

v2 whole, which is shorter than its diff:
```python
import functools

import jax
import jax.numpy as jnp
from jax import lax
from jax.experimental import pallas as pl
from jax.experimental.pallas import tpu as pltpu
from jax.sharding import PartitionSpec as P

MESH = pl.DeviceIdType.MESH
ROOT = 0.7978845608028654
CUBIC = 0.044715
W = 128
KEEP = 6
FOOT = 8
F32 = jnp.float32
BF16 = jnp.bfloat16


def gelu_pair(values):
    inside = ROOT * (values + CUBIC * values * values * values)
    tangent = jnp.tanh(inside)
    activated = 0.5 * values * (1.0 + tangent)
    derivative = 0.5 * (1.0 + tangent) + 0.5 * values * (1.0 - tangent * tangent) * ROOT * (
        1.0 + 3.0 * CUBIC * values * values
    )
    return activated, derivative


def coded(part):
    most = jnp.maximum(jnp.max(jnp.abs(part), axis=0, keepdims=True), 1e-30)
    power = jnp.floor(jnp.log(most) * 1.4426950408889634) + 1.0
    units = jnp.round(part * jnp.exp2(15.0 - power))
    units = jnp.clip(units, -32767.0, 32767.0).astype(jnp.int32).astype(jnp.int16)
    foot = jnp.broadcast_to(power, (FOOT, part.shape[1])).astype(jnp.int32).astype(jnp.int16)
    return units, foot


def store_coded(tile, lanes, part):
    rows = part.shape[0]
    units, foot = coded(part)
    tile[pl.ds(0, rows), lanes] = units
    tile[pl.ds(rows, FOOT), lanes] = foot


def decoded(tile, rows, lanes):
    power = tile[pl.ds(rows, FOOT), lanes].astype(jnp.int32).astype(F32)[0:1]
    units = tile[pl.ds(0, rows), lanes].astype(jnp.int32).astype(F32)
    return units * jnp.exp2(power - 15.0)


def kernel(
    dims,
    codes, scales, mask, cot, wg, wu, wo,
    dx_out, own_out, got_out,
    sl, wc, pb, r1, r2, guh, dx, dws, dwr, relay, dxs, dxr, ybuf, y2, zbuf,
    w_sem, ag_s, ag_r, rs1_s, rs1_r, rs2_s, rs2_r, a1_s, a1_r, a2_s, a2_r,
    p1_s, p1_r, p2_s, p2_r, own_sem, got_sem, dxc_s, dxc_r, y1_s, y1_r, y2_s, y2_r, z_s, z_r,
):
    tb, dl, chunks = dims
    blk = 4 * tb
    units = 4 * chunks
    x = lax.axis_index("row")
    col = lax.axis_index("col")
    dp = lax.axis_index("dp")
    core = lax.rem(col, 2)
    y = lax.rem(col // 2, 4)
    z = col // 8
    opp = lax.rem(x + 2, 4)

    def at_col(dz, dy, dc):
        zz = (1 - z) if dz else z
        cc = (1 - core) if dc else core
        return {"col": (zz * 4 + lax.rem(y + dy, 4)) * 2 + cc}

    def beside(way):
        return lax.rem(x + 1 + 2 * way, 4)

    def to_row(way):
        return {"row": beside(way)}

    partner = at_col(0, 0, 1)
    up, down = at_col(0, 1, 0), at_col(0, 3, 0)
    near = at_col(1, 0, 0)
    far = dict(near, dp=1 - dp)

    barrier = pltpu.get_barrier_semaphore()
    peers = [to_row(0), to_row(1), partner, up, down, near, far]
    for peer in peers:
        pl.semaphore_signal(barrier, inc=1, device_id=peer, device_id_type=MESH)

    def weight_copy(j, m, src):
        return pltpu.make_async_copy(
            src.at[:, pl.ds(j * W, W)], wc.at[j, :, pl.ds(m * W, W)], w_sem.at[j, m]
        )

    for j in range(chunks):
        for m, src in enumerate((wg, wu, wo)):
            weight_copy(j, m, src).start()

    nb = scales.shape[0]
    flat = jnp.concatenate(
        [scales[...].astype(F32), jnp.broadcast_to(mask[...], (8, tb)).astype(F32),
         jnp.zeros((128 - nb - 8, tb), F32)], axis=0,
    )
    tall = jnp.transpose(flat)
    for k in range(nb):
        lanes = pl.ds(k * 128, 128)
        level = (2 * codes[:, lanes] - 3).astype(F32) * tall[:, k : k + 1]
        sl[pl.ds(0, tb), lanes] = (level * 0.0625).astype(BF16)
        live = cot[:, lanes].astype(F32) * tall[:, nb : nb + 1]
        sl[pl.ds(0, tb), pl.ds(dl + k * 128, 128)] = live.astype(BF16)

    with jax.named_scope("barrier"):
        pl.semaphore_wait(barrier, len(peers))

    def remote(src, dst, s_sem, r_sem, device):
        return pltpu.make_async_remote_copy(
            src_ref=src, dst_ref=dst, send_sem=s_sem, recv_sem=r_sem,
            device_id=device, device_id_type=MESH,
        )

    def slot(b, zr, cr):
        return (b * 4 + zr * 2 + cr) * tb

    def rows(start, count):
        return sl.at[pl.ds(start, count)]

    started = []

    def gather(kind, src, dst, count, device):
        copy = remote(rows(src, count), rows(dst, count), ag_s.at[kind], ag_r.at[kind], device)
        copy.start()
        started.append(copy)

    def arrived(kind, dst, count):
        remote(rows(dst, count), rows(dst, count), ag_s.at[kind], ag_r.at[kind], partner).wait_recv()

    def to_core(kind, b, zr):
        gather(9 + kind, slot(b, zr, 0), slot(b, zr, 1), tb, partner)

    part = tb // 2
    gather(0, slot(0, 0, 0), slot(0, 1, 0), tb, near)
    gather(1, slot(0, 0, 0), slot(1, 0, 0), tb, up)
    gather(2, slot(0, 0, 0), slot(2, 0, 0), tb, down)
    to_core(0, 0, 0)
    for j in range(chunks):
        for m, src in enumerate((wg, wu, wo)):
            weight_copy(j, m, src).wait()

    def unit(u):
        s = (u // 8 + 1) // 2
        return (1 - s) * lax.rem(u, 2) + s * (u // 4), (1 - s) * (u // 2) + s * lax.rem(u, 4)

    def unit_of(j, b):
        s = (j // 2 + 1) // 2
        return (1 - s) * (2 * b + j) + s * (4 * j + b)

    def held(u):
        return pb.at[lax.rem(u, KEEP)]

    def grad_rows(j, b, owner):
        return guh.at[j, pl.ds(pl.multiple_of((b * 4 + owner) * tb, tb), tb)]

    def rs1(u, way):
        return remote(held(u).at[opp], r1.at[u], rs1_s.at[u], rs1_r.at[u], to_row(way))

    def rs2(u, way):
        return remote(
            held(u).at[beside(way)], r2.at[u, way], rs2_s.at[u, way], rs2_r.at[u, way], to_row(way)
        )

    def a1(u, way, owner):
        j, b = unit(u)
        ref = grad_rows(j, b, owner)
        return remote(ref, ref, a1_s.at[u, way], a1_r.at[u, way], to_row(way))

    def a2(u, owner):
        j, b = unit(u)
        ref = grad_rows(j, b, owner)
        return remote(ref, ref, a2_s.at[u], a2_r.at[u], to_row(lax.rem(b, 2)))

    def sent(u):
        rs1(u, lax.rem(unit(u)[1], 2)).wait_send()
        for way in range(2):
            rs2(u, way).wait_send()

    def stage_f(u):
        j, b = unit(u)
        if isinstance(u, int):
            if u >= KEEP:
                sent(u - KEEP)
        else:
            sent(u - KEEP)
        where = pl.ds(pl.multiple_of(b * blk, blk), blk)
        both = jnp.dot(
            sl[where, pl.ds(0, dl)], wc[j, :, pl.ds(0, 2 * W)], preferred_element_type=F32
        )
        back = jnp.dot(
            sl[where, pl.ds(dl, dl)], wc[j, :, pl.ds(2 * W, W)], preferred_element_type=F32
        )
        for o in range(4):
            tile = held(u).at[o]
            store_coded(tile, pl.ds(0, 2 * W), both[o * tb : (o + 1) * tb])
            store_coded(tile, pl.ds(2 * W, W), back[o * tb : (o + 1) * tb])
        rs1(u, lax.rem(b, 2)).start()

    def stage_r(u):
        j, b = unit(u)
        way = lax.rem(b, 2)
        rs2(u, 1 - way).start()
        with jax.named_scope("r_wait"):
            rs1(u, way).wait_recv()
        tile = held(u).at[beside(way)]
        for m in range(3):
            lanes = pl.ds(m * W, W)
            total = decoded(tile, tb, lanes) + decoded(r1.at[u], tb, lanes)
            store_coded(tile, lanes, total)
        rs2(u, way).start()

    def stage_a(u):
        j, b = unit(u)
        with jax.named_scope("a_wait"):
            for way in range(2):
                rs2(u, way).wait_recv()
        tiles = (held(u).at[x], r2.at[u, 0], r2.at[u, 1])
        powers = [
            [
                jnp.exp2(t[pl.ds(tb, FOOT), pl.ds(m * W, W)].astype(jnp.int32).astype(F32)[0:1] - 15.0)
                for t in tiles
            ]
            for m in range(3)
        ]
        step = tb // 2

        def body(k, carry):
            some = pl.ds(pl.multiple_of(k * step, step), step)
            sums = []
            for m in range(3):
                total = None
                for t, power in zip(tiles, powers[m]):
                    term = t[some, pl.ds(m * W, W)].astype(jnp.int32).astype(F32) * power
                    total = term if total is None else total + term
                sums.append(total)
            gate, up_part, back = sums
            activated, derivative = gelu_pair(gate)
            to = pl.ds(pl.multiple_of((b * 4 + x) * tb + k * step, step), step)
            guh[j, to, pl.ds(0, W)] = (back * up_part * derivative).astype(BF16)
            guh[j, to, pl.ds(W, W)] = (back * activated).astype(BF16)
            guh[j, to, pl.ds(2 * W, W)] = (activated * up_part).astype(BF16)
            return carry

        lax.fori_loop(0, 2, body, 0)
        for way in range(2):
            a1(u, way, x).start()

    def stage_w(u):
        b = unit(u)[1]
        way = lax.rem(b, 2)
        with jax.named_scope("w_wait"):
            a1(u, way, beside(1 - way)).wait_recv()
        a2(u, beside(1 - way)).start()

    def stage_dx(j):
        with jax.named_scope("b_wait"):
            for b in range(4):
                u = unit_of(j, b)
                a1(u, 1 - b % 2, beside(b % 2)).wait_recv()
                a2(u, opp).wait_recv()

        def body(k, carry):
            where = pl.ds(pl.multiple_of(k * 2 * tb, 2 * tb), 2 * tb)
            more = lax.dot_general(
                guh[j, where, pl.ds(0, 2 * W)], wc[j, :, pl.ds(0, 2 * W)],
                (((1,), (1,)), ((), ())), preferred_element_type=F32,
            )
            dx[where, :] = dx[where, :] + more
            return carry

        lax.fori_loop(0, 8, body, 0)

    half = dl // 2

    def p1(j, way):
        part_of = dws.at[j, pl.ds(way * half, half)]
        return remote(
            part_of, relay.at[j, way], p1_s.at[j, way], p1_r.at[j, way], (near, far)[way]
        )

    def p2(j, way):
        return remote(
            relay.at[j, way], dwr.at[j, pl.ds(way * half, half)], p2_s.at[j, way],
            p2_r.at[j, way], (far, near)[way],
        )

    def own_copy(j):
        return pltpu.make_async_copy(dws.at[j], own_out.at[j], own_sem.at[j])

    def got_copy(j):
        return pltpu.make_async_copy(dwr.at[j], got_out.at[j], got_sem.at[j])

    def stage_dw(j):
        def body(k, carry):
            where = pl.ds(pl.multiple_of(k * 256, 256), 256)
            some = lax.dot_general(
                sl[:, where], guh[j, :, pl.ds(0, 2 * W)],
                (((0,), (0,)), ((), ())), preferred_element_type=F32,
            )
            dws[j, where, pl.ds(0, 2 * W)] = some.astype(BF16)
            last = lax.dot_general(
                sl[:, pl.ds(pl.multiple_of(dl + k * 256, 256), 256)], guh[j, :, pl.ds(2 * W, W)],
                (((0,), (0,)), ((), ())), preferred_element_type=F32,
            )
            dws[j, where, pl.ds(2 * W, W)] = last.astype(BF16)
            return carry

        lax.fori_loop(0, dl // 256, body, 0)
        for way in range(2):
            p1(j, way).start()
        own_copy(j).start()

    def stage_g(j):
        for way in range(2):
            with jax.named_scope("g_wait"):
                p1(j, way).wait_recv()
            p2(j, way).start()

    def stage_e(j):
        with jax.named_scope("e_wait"):
            for way in range(2):
                p2(j, way).wait_recv()
        got_copy(j).start()

    arrived(0, slot(0, 1, 0), tb)
    gather(3, slot(0, 1, 0), slot(1, 1, 0), tb, up)
    gather(4, slot(0, 1, 0), slot(2, 1, 0), tb, down)
    to_core(1, 0, 1)
    arrived(1, slot(1, 0, 0), tb)
    gather(5, slot(1, 0, 0), slot(3, 0, 0), part, up)
    to_core(2, 1, 0)
    arrived(2, slot(2, 0, 0), tb)
    gather(6, slot(2, 0, 0) + part, slot(3, 0, 0) + part, part, down)
    to_core(3, 2, 0)
    arrived(9, slot(0, 0, 1), tb)
    arrived(10, slot(0, 1, 1), tb)

    def run(stage, *which):
        for u in which:
            with jax.named_scope(f"{stage.__name__}_{u}"):
                stage(u)

    run(stage_f, 0, 1)
    run(stage_r, 0, 1)
    run(stage_a, 0, 1)
    with jax.named_scope("ag1"):
        arrived(3, slot(1, 1, 0), tb)
        gather(7, slot(1, 1, 0), slot(3, 1, 0), part, up)
        to_core(4, 1, 1)
        arrived(4, slot(2, 1, 0), tb)
        gather(8, slot(2, 1, 0) + part, slot(3, 1, 0) + part, part, down)
        to_core(5, 2, 1)
    run(stage_w, 0, 1)
    with jax.named_scope("ag2"):
        arrived(11, slot(1, 0, 1), tb)
        arrived(13, slot(1, 1, 1), tb)
        arrived(12, slot(2, 0, 1), tb)
        arrived(14, slot(2, 1, 1), tb)
    run(stage_f, 2, 3, 4, 5)
    run(stage_r, 2, 3)
    run(stage_a, 2, 3)
    run(stage_r, 4, 5)
    with jax.named_scope("ag3"):
        arrived(5, slot(3, 0, 0), part)
        arrived(6, slot(3, 0, 0) + part, part)
        to_core(6, 3, 0)
        arrived(7, slot(3, 1, 0), part)
        arrived(8, slot(3, 1, 0) + part, part)
        to_core(7, 3, 1)
        arrived(15, slot(3, 0, 1), tb)
        arrived(16, slot(3, 1, 1), tb)
    run(stage_f, 6, 7)
    dx[...] = jnp.zeros_like(dx)

    last = chunks - 1

    def step(t, carry):
        def at(lag, fn, least=0, most=units):
            @pl.when(jnp.logical_and(t - lag >= least, t - lag < most))
            def _():
                with jax.named_scope(fn.__name__):
                    fn(t - lag)

        def at_end(lag, *fns):
            j, b = unit(t - lag)

            @pl.when(jnp.logical_and(jnp.logical_and(t - lag >= 0, b == 3), j < last))
            def _():
                for fn in fns:
                    with jax.named_scope(fn.__name__):
                        fn(j)

        at(0, stage_f)
        at(2, stage_r)
        at(4, stage_a)
        at(6, stage_w)
        at_end(8, stage_dx, stage_dw)
        at_end(11, stage_g)
        at_end(14, stage_e)
        return carry

    lax.fori_loop(8, units + 7, step, 0)

    with jax.named_scope("dx_last"):
        stage_dx(last)

    def dx_rows(b, zr, cr):
        return pl.ds(slot(b, zr, cr), tb)

    def core_copy(b):
        return remote(dxs.at[b], dxr.at[b], dxc_s.at[b], dxc_r.at[b], partner)

    for b in (3, 1, 2, 0):
        for zr in range(2):
            dxs[b, zr] = dx[dx_rows(b, zr, 1), :].astype(BF16)
        core_copy(b).start()
    with jax.named_scope("dw_last"):
        stage_dw(last)

    def y1_copy(zr):
        return remote(dxs.at[3, zr], ybuf.at[zr], y1_s.at[zr], y1_r.at[zr], (up, down)[zr])

    def y2_copy(way, zr):
        return remote(
            dxs.at[2 - way, zr], y2.at[way, zr], y2_s.at[way, zr], y2_r.at[way, zr],
            (up, down)[way],
        )

    core_copy(3).wait()
    for zr in range(2):
        dxs[3, zr] = (dx[dx_rows(3, zr, 0), :] + dxr[3, zr].astype(F32)).astype(BF16)
        y1_copy(zr).start()
    for way in range(2):
        b, zr = 2 - way, 1 - way
        core_copy(b).wait()
        dxs[b, zr] = (dx[dx_rows(b, zr, 0), :] + dxr[b, zr].astype(F32)).astype(BF16)
        y2_copy(way, zr).start()
    with jax.named_scope("y1_wait"):
        for way in range(2):
            y1_copy(way).wait_recv()
            b, zr = 2 - way, way
            total = dx[dx_rows(b, zr, 0), :] + dxr[b, zr].astype(F32) + ybuf[zr].astype(F32)
            dxs[b, zr] = total.astype(BF16)
            y2_copy(way, zr).start()
    core_copy(0).wait()
    for zr in range(2):
        dx[dx_rows(0, zr, 0), :] = dx[dx_rows(0, zr, 0), :] + dxr[0, zr].astype(F32)
    with jax.named_scope("g_last"):
        stage_g(last)
    with jax.named_scope("e_prev"):
        stage_e(last - 1)
    z_copy = remote(dxs.at[0, 1], zbuf, z_s.at[0], z_r.at[0], near)
    with jax.named_scope("y2_wait"):
        for way in range(2):
            y2_copy(way, 1).wait_recv()
        total = dx[dx_rows(0, 1, 0), :] + y2[0, 1].astype(F32) + y2[1, 1].astype(F32)
        dxs[0, 1] = total.astype(BF16)
        z_copy.start()
        for way in range(2):
            y2_copy(way, 0).wait_recv()
        total = dx[dx_rows(0, 0, 0), :] + y2[0, 0].astype(F32) + y2[1, 0].astype(F32)
    with jax.named_scope("z_wait"):
        z_copy.wait()
    dx_out[...] = total + zbuf[...].astype(F32)
    with jax.named_scope("e_last"):
        stage_e(last)

    with jax.named_scope("end"):
        for copy in started:
            copy.wait_send()
        for u in range(units - KEEP, units):
            sent(u)
        for u in range(units):
            for way in range(2):
                a1(u, way, x).wait_send()
            a2(u, opp).wait_send()
        for j in range(chunks):
            for way in range(2):
                p1(j, way).wait_send()
                p2(j, way).wait_send()
            own_copy(j).wait()
            got_copy(j).wait()
        for zr in range(2):
            y1_copy(zr).wait_send()
            for way in range(2):
                y2_copy(way, zr).wait_send()


def combine(own, got, dx, dx_out, g_out, u_out, o_out):
    for j in range(own.shape[0]):
        for m, out in enumerate((g_out, u_out, o_out)):
            lanes = pl.ds(m * W, W)
            out[:, pl.ds(j * W, W)] = own[j, :, lanes].astype(F32) + got[j, :, lanes].astype(F32)
    dx_out[...] = dx[...]


def per_device(codes, scales, mask, cot, wg, wu, wo):
    tb, dl = codes.shape
    fl = wg.shape[1]
    chunks = fl // W
    units = 4 * chunks
    dims = (tb, dl, chunks)
    tile = tb + FOOT
    vmem = pl.BlockSpec(memory_space=pltpu.VMEM)
    hbm = pl.BlockSpec(memory_space=pl.ANY)
    dma = pltpu.SemaphoreType.DMA
    grads = jax.ShapeDtypeStruct((chunks, dl, 3 * W), BF16)
    dx, own, got = pl.pallas_call(
        functools.partial(kernel, dims),
        out_shape=(jax.ShapeDtypeStruct((tb, dl), F32), grads, grads),
        in_specs=[vmem] * 4 + [hbm] * 3,
        out_specs=(vmem, hbm, hbm),
        scratch_shapes=[
            pltpu.VMEM((16 * tb, 2 * dl), BF16),
            pltpu.VMEM((chunks, dl, 3 * W), BF16),
            pltpu.VMEM((KEEP, 4, tile, 3 * W), jnp.int16),
            pltpu.VMEM((units, tile, 3 * W), jnp.int16),
            pltpu.VMEM((units, 2, tile, 3 * W), jnp.int16),
            pltpu.VMEM((chunks, 16 * tb, 3 * W), BF16),
            pltpu.VMEM((16 * tb, dl), F32),
            pltpu.VMEM((chunks, dl, 3 * W), BF16),
            pltpu.VMEM((chunks, dl, 3 * W), BF16),
            pltpu.VMEM((chunks, 2, dl // 2, 3 * W), BF16),
            pltpu.VMEM((4, 2, tb, dl), BF16),
            pltpu.VMEM((4, 2, tb, dl), BF16),
            pltpu.VMEM((2, tb, dl), BF16),
            pltpu.VMEM((2, 2, tb, dl), BF16),
            pltpu.VMEM((tb, dl), BF16),
            dma((chunks, 3)),
            dma((17,)), dma((17,)),
            dma((units,)), dma((units,)),
            dma((units, 2)), dma((units, 2)),
            dma((units, 2)), dma((units, 2)),
            dma((units,)), dma((units,)),
            dma((chunks, 2)), dma((chunks, 2)),
            dma((chunks, 2)), dma((chunks, 2)),
            dma((chunks,)), dma((chunks,)),
            dma((4,)), dma((4,)),
            dma((2,)), dma((2,)),
            dma((2, 2)), dma((2, 2)),
            dma((1,)), dma((1,)),
        ],
        compiler_params=pltpu.CompilerParams(
            collective_id=0, has_side_effects=True, vmem_limit_bytes=67043328
        ),
        name="ffn_backward",
    )(codes, scales.T, mask[None, :], cot, wg, wu, wo)
    weight = jax.ShapeDtypeStruct((dl, fl), F32)
    steps = 8
    rows = dl // steps
    return pl.pallas_call(
        combine,
        grid=(steps,),
        out_shape=(jax.ShapeDtypeStruct((tb, dl), F32), weight, weight, weight),
        in_specs=[
            pl.BlockSpec((chunks, rows, 3 * W), lambda i: (0, i, 0)),
            pl.BlockSpec((chunks, rows, 3 * W), lambda i: (0, i, 0)),
            pl.BlockSpec((tb // steps, dl), lambda i: (i, 0)),
        ],
        out_specs=[pl.BlockSpec((tb // steps, dl), lambda i: (i, 0))]
        + [pl.BlockSpec((rows, fl), lambda i: (i, 0))] * 3,
        name="combine",
    )(own, got, dx)


def solution(mesh):
    tokens = P(("dp", "col"), "row")
    weights = P("row", "col")
    return jax.shard_map(
        per_device,
        mesh=mesh,
        in_specs=(tokens, tokens, P(("dp", "col")), tokens, weights, weights, weights),
        out_specs=(tokens, weights, weights, weights),
        check_vma=False,
    )
```

time: 260 us -> 219 us (0.84)
  Pallas kernels: 245 us -> 217 us
  local copies, waits for them, and re-layouts: 12.4 us -> 0 us
    pallas_call x1, Pallas kernels: 245 us -> 208 us  [per_device(): pl.pallas_call(functools.partial(kernel, dims), out_shape=(jax.ShapeDtype...]
    unnamed x9 -> x0, local copies, waits for them, and re-layouts: 11 us -> none
    pallas_call x0 -> x1, Pallas kernels: none -> 8.69 us  [per_device(): pl.pallas_call(combine, grid=(steps,), out_shape=(jax.ShapeDtypeStruct((t...]
where the time goes in v2:
time: 219 us; the launch traced here: 217 us
  Pallas kernels  217 us (99%)
    pallas_call x1, Pallas kernels, per_device(): pl.pallas_call(functools.partial(kernel, dims), out_shape=(jax.ShapeDtype...  208 us
    pallas_call x1, Pallas kernels, per_device(): pl.pallas_call(combine, grid=(steps,), out_shape=(jax.ShapeDtypeStruct((t...  8.69 us

profile of v2, /device:TPU:0, one launch (start us, length us, event | category | flops | bytes accessed | tf_op | source)
XLA Modules:
  0.0 217.2 jit_solution(14506923968149000847)
XLA Ops:
  0.6 207.8 %ffn_backward.1 = (f32[128,1024]{1,0:T(8,128)}, bf16[5,1024,384]{2,1,0:T(8,128)(2,1)}, bf16[5,1024,384]{2,1,0:T(8,128)(2,1)}) custom-call(s32[128,1024]{1,0:T(8,128)} %codes.1, s32[8,128]{1,0:T(8,128)} %bitcast.2, s32[1,128]{1,0:T(1,128)} %bitcast.3, bf16[128,1024]{1,0:T(8,128)(2,1)} %cot.1, bf16[1024,640]{1,0:T(8,128)(2,1)} %wg.1, bf16[1024,640]{1,0:T(8,128)(2,1)} %wu.1, ...), custom_call_target="tpu_custom_call" | custom-call | tf_op jit(solution)/shard_map/ffn_backward/pallas_call | solution.py:517
  208.5 8.7 %combine.1 = (f32[128,1024]{1,0:T(8,128)}, f32[1024,640]{1,0:T(8,128)}, f32[1024,640]{1,0:T(8,128)}, f32[1024,640]{1,0:T(8,128)}) custom-call(bf16[5,1024,384]{2,1,0:T(8,128)(2,1)} %get-tuple-element.7.own, bf16[5,1024,384]{2,1,0:T(8,128)(2,1)} %get-tuple-element.8.got, f32[128,1024]{1,0:T(8,128)} %get-tuple-element.9.dx), custom_call_target="tpu_custom_call" | custom-call | tf_op jit(solution)/shard_map/combine/pallas_call | solution.py:560

commit v3 on v2

--- a/solution.py
+++ b/solution.py
@@ -148,13 +148,13 @@
         for m, src in enumerate((wg, wu, wo)):
             weight_copy(j, m, src).wait()
 
+    def place(u):
+        s = (u // 8 + 1) // 2
+        return s, (1 - s) * (u // 2) + s * lax.rem(u, 4)
+
     def unit(u):
-        s = (u // 8 + 1) // 2
-        return (1 - s) * lax.rem(u, 2) + s * (u // 4), (1 - s) * (u // 2) + s * lax.rem(u, 4)
-
-    def unit_of(j, b):
-        s = (j // 2 + 1) // 2
-        return (1 - s) * (2 * b + j) + s * (4 * j + b)
+        s, k = place(u)
+        return (1 - s) * lax.rem(u, 2) + s * (u // 4), (1 - s) * k + s * (3 - k)
 
     def held(u):
         return pb.at[lax.rem(u, KEEP)]
@@ -261,23 +261,18 @@
             a1(u, way, beside(1 - way)).wait_recv()
         a2(u, beside(1 - way)).start()
 
-    def stage_dx(j):
+    def stage_dx(u):
+        j, b = unit(u)
+        way = lax.rem(b, 2)
         with jax.named_scope("b_wait"):
-            for b in range(4):
-                u = unit_of(j, b)
-                a1(u, 1 - b % 2, beside(b % 2)).wait_recv()
-                a2(u, opp).wait_recv()
-
-        def body(k, carry):
-            where = pl.ds(pl.multiple_of(k * 2 * tb, 2 * tb), 2 * tb)
-            more = lax.dot_general(
-                guh[j, where, pl.ds(0, 2 * W)], wc[j, :, pl.ds(0, 2 * W)],
-                (((1,), (1,)), ((), ())), preferred_element_type=F32,
-            )
-            dx[where, :] = dx[where, :] + more
-            return carry
-
-        lax.fori_loop(0, 8, body, 0)
+            a1(u, 1 - way, beside(way)).wait_recv()
+            a2(u, opp).wait_recv()
+        where = pl.ds(pl.multiple_of(b * blk, blk), blk)
+        more = lax.dot_general(
+            guh[j, where, pl.ds(0, 2 * W)], wc[j, :, pl.ds(0, 2 * W)],
+            (((1,), (1,)), ((), ())), preferred_element_type=F32,
+        )
+        dx[where, :] = dx[where, :] + more
 
     half = dl // 2
 
@@ -330,6 +325,8 @@
             for way in range(2):
                 p2(j, way).wait_recv()
         got_copy(j).start()
+
+    dx[...] = jnp.zeros_like(dx)
 
     arrived(0, slot(0, 1, 0), tb)
     gather(3, slot(0, 1, 0), slot(1, 1, 0), tb, up)
@@ -379,52 +376,44 @@
         arrived(15, slot(3, 0, 1), tb)
         arrived(16, slot(3, 1, 1), tb)
     run(stage_f, 6, 7)
-    dx[...] = jnp.zeros_like(dx)
+    run(stage_w, 2, 3)
+    run(stage_a, 4, 5)
+    run(stage_r, 6)
+    run(stage_w, 4)
+    run(stage_dx, 0, 1, 2, 3)
 
     last = chunks - 1
 
     def step(t, carry):
-        def at(lag, fn, least=0, most=units):
-            @pl.when(jnp.logical_and(t - lag >= least, t - lag < most))
+        def at(lag, fn):
+            with jax.named_scope(fn.__name__):
+                fn(t - lag)
+
+        def at_end(lag, fn):
+            j = unit(t - lag)[0]
+
+            @pl.when(jnp.logical_and(t - lag >= 0, place(t - lag)[1] == 3))
             def _():
                 with jax.named_scope(fn.__name__):
-                    fn(t - lag)
-
-        def at_end(lag, *fns):
-            j, b = unit(t - lag)
-
-            @pl.when(jnp.logical_and(jnp.logical_and(t - lag >= 0, b == 3), j < last))
-            def _():
-                for fn in fns:
-                    with jax.named_scope(fn.__name__):
-                        fn(j)
+                    fn(j)
 
         at(0, stage_f)
-        at(2, stage_r)
-        at(4, stage_a)
-        at(6, stage_w)
-        at_end(8, stage_dx, stage_dw)
-        at_end(11, stage_g)
-        at_end(14, stage_e)
+        at(1, stage_r)
+        at(2, stage_a)
+        at(3, stage_w)
+        at(4, stage_dx)
+        at_end(4, stage_dw)
+        at_end(7, stage_g)
+        at_end(10, stage_e)
         return carry
 
-    lax.fori_loop(8, units + 7, step, 0)
-
-    with jax.named_scope("dx_last"):
-        stage_dx(last)
+    lax.fori_loop(8, units, step, 0)
 
     def dx_rows(b, zr, cr):
         return pl.ds(slot(b, zr, cr), tb)
 
     def core_copy(b):
         return remote(dxs.at[b], dxr.at[b], dxc_s.at[b], dxc_r.at[b], partner)
-
-    for b in (3, 1, 2, 0):
-        for zr in range(2):
-            dxs[b, zr] = dx[dx_rows(b, zr, 1), :].astype(BF16)
-        core_copy(b).start()
-    with jax.named_scope("dw_last"):
-        stage_dw(last)
 
     def y1_copy(zr):
         return remote(dxs.at[3, zr], ybuf.at[zr], y1_s.at[zr], y1_r.at[zr], (up, down)[zr])
@@ -435,44 +424,69 @@
             (up, down)[way],
         )
 
+    def send_core(b):
+        for zr in range(2):
+            dxs[b, zr] = dx[dx_rows(b, zr, 1), :].astype(BF16)
+        core_copy(b).start()
+
+    def chip_sum(b, zr):
+        return dx[dx_rows(b, zr, 0), :] + dxr[b, zr].astype(F32)
+
+    def ring_step(way):
+        b, zr = 2 - way, way
+        with jax.named_scope("core_wait"):
+            core_copy(b).wait()
+        dxs[b, 1 - zr] = chip_sum(b, 1 - zr).astype(BF16)
+        y2_copy(way, 1 - zr).start()
+        with jax.named_scope("y1_wait"):
+            y1_copy(zr).wait_recv()
+        dxs[b, zr] = (chip_sum(b, zr) + ybuf[zr].astype(F32)).astype(BF16)
+        y2_copy(way, zr).start()
+
+    run(stage_r, units - 1)
+    run(stage_a, units - 2)
+    run(stage_w, units - 3)
+    run(stage_dx, units - 4)
+    send_core(3)
+    run(stage_a, units - 1)
+    run(stage_w, units - 2)
+    run(stage_dx, units - 3)
+    send_core(2)
     core_copy(3).wait()
     for zr in range(2):
-        dxs[3, zr] = (dx[dx_rows(3, zr, 0), :] + dxr[3, zr].astype(F32)).astype(BF16)
+        dxs[3, zr] = chip_sum(3, zr).astype(BF16)
         y1_copy(zr).start()
-    for way in range(2):
-        b, zr = 2 - way, 1 - way
-        core_copy(b).wait()
-        dxs[b, zr] = (dx[dx_rows(b, zr, 0), :] + dxr[b, zr].astype(F32)).astype(BF16)
-        y2_copy(way, zr).start()
-    with jax.named_scope("y1_wait"):
-        for way in range(2):
-            y1_copy(way).wait_recv()
-            b, zr = 2 - way, way
-            total = dx[dx_rows(b, zr, 0), :] + dxr[b, zr].astype(F32) + ybuf[zr].astype(F32)
-            dxs[b, zr] = total.astype(BF16)
-            y2_copy(way, zr).start()
+    run(stage_w, units - 1)
+    run(stage_dx, units - 2)
+    send_core(1)
+    ring_step(0)
+    ring_step(1)
+    run(stage_dx, units - 1)
+    send_core(0)
+    run(stage_g, last - 1)
+    run(stage_dw, last)
     core_copy(0).wait()
     for zr in range(2):
-        dx[dx_rows(0, zr, 0), :] = dx[dx_rows(0, zr, 0), :] + dxr[0, zr].astype(F32)
-    with jax.named_scope("g_last"):
-        stage_g(last)
-    with jax.named_scope("e_prev"):
-        stage_e(last - 1)
+        dx[dx_rows(0, zr, 0), :] = chip_sum(0, zr)
     z_copy = remote(dxs.at[0, 1], zbuf, z_s.at[0], z_r.at[0], near)
     with jax.named_scope("y2_wait"):
         for way in range(2):
             y2_copy(way, 1).wait_recv()
-        total = dx[dx_rows(0, 1, 0), :] + y2[0, 1].astype(F32) + y2[1, 1].astype(F32)
-        dxs[0, 1] = total.astype(BF16)
-        z_copy.start()
-        for way in range(2):
-            y2_copy(way, 0).wait_recv()
-        total = dx[dx_rows(0, 0, 0), :] + y2[0, 0].astype(F32) + y2[1, 0].astype(F32)
+    total = dx[dx_rows(0, 1, 0), :] + y2[0, 1].astype(F32) + y2[1, 1].astype(F32)
+    dxs[0, 1] = total.astype(BF16)
+    z_copy.start()
+    run(stage_e, last - 2)
+    for way in range(2):
+        y2_copy(way, 0).wait_recv()
+    dx[dx_rows(0, 0, 0), :] = (
+        dx[dx_rows(0, 0, 0), :] + y2[0, 0].astype(F32) + y2[1, 0].astype(F32)
+    )
+    run(stage_g, last)
+    run(stage_e, last - 1)
     with jax.named_scope("z_wait"):
         z_copy.wait()
-    dx_out[...] = total + zbuf[...].astype(F32)
-    with jax.named_scope("e_last"):
-        stage_e(last)
+    dx_out[...] = dx[dx_rows(0, 0, 0), :] + zbuf[...].astype(F32)
+    run(stage_e, last)
 
     with jax.named_scope("end"):
         for copy in started:

time: 219 us -> 216 us (0.986)
  no operation moved by 1% of the time
where the time goes in v3:
time: 216 us
  Pallas kernels  215 us (100%)
    pallas_call x1, Pallas kernels, per_device(): pl.pallas_call(functools.partial(kernel, dims), out_shape=(jax.ShapeDtype...  207 us
    pallas_call x1, Pallas kernels, per_device(): pl.pallas_call(combine, grid=(steps,), out_shape=(jax.ShapeDtypeStruct((t...  8.69 us

profile of v3, /device:TPU:0, one launch (start us, length us, event | category | flops | bytes accessed | tf_op | source)
XLA Modules:
  0.0 215.9 jit_solution(15938126247304533071)
XLA Ops:
  0.6 206.6 %ffn_backward.1 = (f32[128,1024]{1,0:T(8,128)}, bf16[5,1024,384]{2,1,0:T(8,128)(2,1)}, bf16[5,1024,384]{2,1,0:T(8,128)(2,1)}) custom-call(s32[128,1024]{1,0:T(8,128)} %codes.1, s32[8,128]{1,0:T(8,128)} %bitcast.2, s32[1,128]{1,0:T(1,128)} %bitcast.3, bf16[128,1024]{1,0:T(8,128)(2,1)} %cot.1, bf16[1024,640]{1,0:T(8,128)(2,1)} %wg.1, bf16[1024,640]{1,0:T(8,128)(2,1)} %wu.1, ...), custom_call_target="tpu_custom_call" | custom-call | tf_op jit(solution)/shard_map/ffn_backward/pallas_call | solution.py:531
  207.2 8.7 %combine.1 = (f32[128,1024]{1,0:T(8,128)}, f32[1024,640]{1,0:T(8,128)}, f32[1024,640]{1,0:T(8,128)}, f32[1024,640]{1,0:T(8,128)}) custom-call(bf16[5,1024,384]{2,1,0:T(8,128)(2,1)} %get-tuple-element.7.own, bf16[5,1024,384]{2,1,0:T(8,128)(2,1)} %get-tuple-element.8.got, f32[128,1024]{1,0:T(8,128)} %get-tuple-element.9.dx), custom_call_target="tpu_custom_call" | custom-call | tf_op jit(solution)/shard_map/combine/pallas_call | solution.py:574

commit v4 on v3

--- a/solution.py
+++ b/solution.py
@@ -53,7 +53,7 @@
     dims,
     codes, scales, mask, cot, wg, wu, wo,
     dx_out, own_out, got_out,
-    sl, wc, pb, r1, r2, guh, dx, dws, dwr, relay, dxs, dxr, ybuf, y2, zbuf,
+    sl, wc, pb, r1, r2, guh, dx, acc, dws, dwr, relay, dxs, dxr, ybuf, y2, zbuf,
     w_sem, ag_s, ag_r, rs1_s, rs1_r, rs2_s, rs2_r, a1_s, a1_r, a2_s, a2_r,
     p1_s, p1_r, p2_s, p2_r, own_sem, got_sem, dxc_s, dxc_r, y1_s, y1_r, y2_s, y2_r, z_s, z_r,
 ):
@@ -150,11 +150,11 @@
 
     def place(u):
         s = (u // 8 + 1) // 2
-        return s, (1 - s) * (u // 2) + s * lax.rem(u, 4)
+        k = (1 - s) * (u // 2) + s * lax.rem(u, 4)
+        return (1 - s) * lax.rem(u, 2) + s * (u // 4), (1 - s) * k + s * (3 - k), k
 
     def unit(u):
-        s, k = place(u)
-        return (1 - s) * lax.rem(u, 2) + s * (u // 4), (1 - s) * k + s * (3 - k)
+        return place(u)[:2]
 
     def held(u):
         return pb.at[lax.rem(u, KEEP)]
@@ -261,12 +261,15 @@
             a1(u, way, beside(1 - way)).wait_recv()
         a2(u, beside(1 - way)).start()
 
-    def stage_dx(u):
+    def arrive_dx(u):
         j, b = unit(u)
         way = lax.rem(b, 2)
         with jax.named_scope("b_wait"):
             a1(u, 1 - way, beside(way)).wait_recv()
             a2(u, opp).wait_recv()
+
+    def add_dx(u):
+        j, b = unit(u)
         where = pl.ds(pl.multiple_of(b * blk, blk), blk)
         more = lax.dot_general(
             guh[j, where, pl.ds(0, 2 * W)], wc[j, :, pl.ds(0, 2 * W)],
@@ -274,18 +277,27 @@
         )
         dx[where, :] = dx[where, :] + more
 
-    half = dl // 2
-
-    def p1(j, way):
-        part_of = dws.at[j, pl.ds(way * half, half)]
+    def stage_dx(u):
+        arrive_dx(u)
+        add_dx(u)
+
+    quarter = dl // 4
+
+    def to_z(other):
+        return dict(near, dp=dp + other * (1 - 2 * dp))
+
+    def piece(k):
+        return pl.ds(pl.multiple_of(k * quarter, quarter), quarter)
+
+    def p1(j, k):
         return remote(
-            part_of, relay.at[j, way], p1_s.at[j, way], p1_r.at[j, way], (near, far)[way]
-        )
-
-    def p2(j, way):
+            dws.at[j, piece(k)], relay.at[j, piece(k)], p1_s.at[j, k], p1_r.at[j, k], to_z(k // 2)
+        )
+
+    def p2(j, k):
         return remote(
-            relay.at[j, way], dwr.at[j, pl.ds(way * half, half)], p2_s.at[j, way],
-            p2_r.at[j, way], (far, near)[way],
+            relay.at[j, piece(k)], dwr.at[j, piece(k)], p2_s.at[j, k], p2_r.at[j, k],
+            to_z(1 - k // 2),
         )
 
     def own_copy(j):
@@ -294,39 +306,53 @@
     def got_copy(j):
         return pltpu.make_async_copy(dwr.at[j], got_out.at[j], got_sem.at[j])
 
-    def stage_dw(j):
-        def body(k, carry):
-            where = pl.ds(pl.multiple_of(k * 256, 256), 256)
+    def stage_dw(u):
+        j, b, k = place(u)
+        where = pl.ds(pl.multiple_of(b * blk, blk), blk)
+        sums = acc.at[lax.rem(j, 2)]
+
+        def body(i, carry):
+            q = lax.rem(i, 2) * 2 + i // 2
             some = lax.dot_general(
-                sl[:, where], guh[j, :, pl.ds(0, 2 * W)],
+                sl[where, piece(q)], guh[j, where, pl.ds(0, 2 * W)],
                 (((0,), (0,)), ((), ())), preferred_element_type=F32,
             )
-            dws[j, where, pl.ds(0, 2 * W)] = some.astype(BF16)
-            last = lax.dot_general(
-                sl[:, pl.ds(pl.multiple_of(dl + k * 256, 256), 256)], guh[j, :, pl.ds(2 * W, W)],
+            more = lax.dot_general(
+                sl[where, pl.ds(pl.multiple_of(dl + q * quarter, quarter), quarter)],
+                guh[j, where, pl.ds(2 * W, W)],
                 (((0,), (0,)), ((), ())), preferred_element_type=F32,
             )
-            dws[j, where, pl.ds(2 * W, W)] = last.astype(BF16)
+            sums[piece(q), pl.ds(0, 2 * W)] = sums[piece(q), pl.ds(0, 2 * W)] + some
+            sums[piece(q), pl.ds(2 * W, W)] = sums[piece(q), pl.ds(2 * W, W)] + more
+
+            @pl.when(k == 3)
+            def _():
+                dws[j, piece(q), :] = sums[piece(q), :].astype(BF16)
+                sums[piece(q), :] = jnp.zeros((quarter, 3 * W), F32)
+                p1(j, q).start()
+
             return carry
 
-        lax.fori_loop(0, dl // 256, body, 0)
-        for way in range(2):
-            p1(j, way).start()
-        own_copy(j).start()
+        lax.fori_loop(0, 4, body, 0)
+
+        @pl.when(k == 3)
+        def _():
+            own_copy(j).start()
 
     def stage_g(j):
-        for way in range(2):
+        for k in (0, 2, 1, 3):
             with jax.named_scope("g_wait"):
-                p1(j, way).wait_recv()
-            p2(j, way).start()
+                p1(j, k).wait_recv()
+            p2(j, k).start()
 
     def stage_e(j):
         with jax.named_scope("e_wait"):
-            for way in range(2):
-                p2(j, way).wait_recv()
+            for k in (0, 2, 1, 3):
+                p2(j, k).wait_recv()
         got_copy(j).start()
 
     dx[...] = jnp.zeros_like(dx)
+    acc[...] = jnp.zeros_like(acc)
 
     arrived(0, slot(0, 1, 0), tb)
     gather(3, slot(0, 1, 0), slot(1, 1, 0), tb, up)
@@ -348,7 +374,6 @@
 
     run(stage_f, 0, 1)
     run(stage_r, 0, 1)
-    run(stage_a, 0, 1)
     with jax.named_scope("ag1"):
         arrived(3, slot(1, 1, 0), tb)
         gather(7, slot(1, 1, 0), slot(3, 1, 0), part, up)
@@ -356,16 +381,23 @@
         arrived(4, slot(2, 1, 0), tb)
         gather(8, slot(2, 1, 0) + part, slot(3, 1, 0) + part, part, down)
         to_core(5, 2, 1)
-    run(stage_w, 0, 1)
+    run(stage_a, 0, 1)
     with jax.named_scope("ag2"):
         arrived(11, slot(1, 0, 1), tb)
         arrived(13, slot(1, 1, 1), tb)
         arrived(12, slot(2, 0, 1), tb)
         arrived(14, slot(2, 1, 1), tb)
-    run(stage_f, 2, 3, 4, 5)
+    run(stage_f, 2, 3)
+    run(stage_w, 0, 1)
+    run(stage_f, 4, 5)
     run(stage_r, 2, 3)
-    run(stage_a, 2, 3)
-    run(stage_r, 4, 5)
+    run(stage_dx, 0)
+    run(stage_dw, 0)
+    run(stage_a, 2)
+    run(stage_r, 4)
+    run(stage_a, 3)
+    run(stage_r, 5)
+    run(stage_w, 2)
     with jax.named_scope("ag3"):
         arrived(5, slot(3, 0, 0), part)
         arrived(6, slot(3, 0, 0) + part, part)
@@ -376,11 +408,16 @@
         arrived(15, slot(3, 0, 1), tb)
         arrived(16, slot(3, 1, 1), tb)
     run(stage_f, 6, 7)
-    run(stage_w, 2, 3)
-    run(stage_a, 4, 5)
+    run(stage_a, 4)
+    run(stage_w, 3)
     run(stage_r, 6)
+    run(stage_a, 5)
+    run(stage_dx, 1)
+    run(stage_dw, 1)
     run(stage_w, 4)
-    run(stage_dx, 0, 1, 2, 3)
+    for u in (2, 3):
+        run(stage_dx, u)
+        run(stage_dw, u)
 
     last = chunks - 1
 
@@ -390,9 +427,9 @@
                 fn(t - lag)
 
         def at_end(lag, fn):
-            j = unit(t - lag)[0]
-
-            @pl.when(jnp.logical_and(t - lag >= 0, place(t - lag)[1] == 3))
+            j, b, k = place(t - lag)
+
+            @pl.when(k == 3)
             def _():
                 with jax.named_scope(fn.__name__):
                     fn(j)
@@ -402,9 +439,16 @@
         at(2, stage_a)
         at(3, stage_w)
         at(4, stage_dx)
-        at_end(4, stage_dw)
-        at_end(7, stage_g)
-        at_end(10, stage_e)
+        at(4, stage_dw)
+
+        @pl.when(t >= 13)
+        def _():
+            at_end(7, stage_g)
+
+        @pl.when(t >= 16)
+        def _():
+            at_end(10, stage_e)
+
         return carry
 
     lax.fori_loop(8, units, step, 0)
@@ -432,12 +476,15 @@
     def chip_sum(b, zr):
         return dx[dx_rows(b, zr, 0), :] + dxr[b, zr].astype(F32)
 
-    def ring_step(way):
-        b, zr = 2 - way, way
+    def ring_early(way):
+        b, zr = 2 - way, 1 - way
         with jax.named_scope("core_wait"):
             core_copy(b).wait()
-        dxs[b, 1 - zr] = chip_sum(b, 1 - zr).astype(BF16)
-        y2_copy(way, 1 - zr).start()
+        dxs[b, zr] = chip_sum(b, zr).astype(BF16)
+        y2_copy(way, zr).start()
+
+    def ring_late(way):
+        b, zr = 2 - way, way
         with jax.named_scope("y1_wait"):
             y1_copy(zr).wait_recv()
         dxs[b, zr] = (chip_sum(b, zr) + ybuf[zr].astype(F32)).astype(BF16)
@@ -448,23 +495,29 @@
     run(stage_w, units - 3)
     run(stage_dx, units - 4)
     send_core(3)
+    run(stage_dw, units - 4)
     run(stage_a, units - 1)
     run(stage_w, units - 2)
-    run(stage_dx, units - 3)
-    send_core(2)
     core_copy(3).wait()
     for zr in range(2):
         dxs[3, zr] = chip_sum(3, zr).astype(BF16)
         y1_copy(zr).start()
+    run(stage_g, last - 1)
+    run(stage_dx, units - 3)
+    send_core(2)
+    run(stage_dw, units - 3)
     run(stage_w, units - 1)
+    ring_early(0)
     run(stage_dx, units - 2)
     send_core(1)
-    ring_step(0)
-    ring_step(1)
-    run(stage_dx, units - 1)
+    run(stage_dw, units - 2)
+    run(arrive_dx, units - 1)
+    run(stage_dw, units - 1)
+    ring_early(1)
+    ring_late(0)
+    ring_late(1)
+    run(add_dx, units - 1)
     send_core(0)
-    run(stage_g, last - 1)
-    run(stage_dw, last)
     core_copy(0).wait()
     for zr in range(2):
         dx[dx_rows(0, zr, 0), :] = chip_sum(0, zr)
@@ -498,9 +551,9 @@
                 a1(u, way, x).wait_send()
             a2(u, opp).wait_send()
         for j in range(chunks):
-            for way in range(2):
-                p1(j, way).wait_send()
-                p2(j, way).wait_send()
+            for k in range(4):
+                p1(j, k).wait_send()
+                p2(j, k).wait_send()
             own_copy(j).wait()
             got_copy(j).wait()
         for zr in range(2):
@@ -541,9 +594,10 @@
             pltpu.VMEM((units, 2, tile, 3 * W), jnp.int16),
             pltpu.VMEM((chunks, 16 * tb, 3 * W), BF16),
             pltpu.VMEM((16 * tb, dl), F32),
+            pltpu.VMEM((2, dl, 3 * W), F32),
             pltpu.VMEM((chunks, dl, 3 * W), BF16),
             pltpu.VMEM((chunks, dl, 3 * W), BF16),
-            pltpu.VMEM((chunks, 2, dl // 2, 3 * W), BF16),
+            pltpu.VMEM((chunks, dl, 3 * W), BF16),
             pltpu.VMEM((4, 2, tb, dl), BF16),
             pltpu.VMEM((4, 2, tb, dl), BF16),
             pltpu.VMEM((2, tb, dl), BF16),
@@ -555,8 +609,8 @@
             dma((units, 2)), dma((units, 2)),
             dma((units, 2)), dma((units, 2)),
             dma((units,)), dma((units,)),
-            dma((chunks, 2)), dma((chunks, 2)),
-            dma((chunks, 2)), dma((chunks, 2)),
+            dma((chunks, 4)), dma((chunks, 4)),
+            dma((chunks, 4)), dma((chunks, 4)),
             dma((chunks,)), dma((chunks,)),
             dma((4,)), dma((4,)),
             dma((2,)), dma((2,)),

time: 216 us -> 213 us (0.986); the launches traced: 216 us -> 210 us
  Pallas kernels: 215 us -> 209 us
    pallas_call x1, Pallas kernels: 207 us -> 200 us  [per_device(): pl.pallas_call(functools.partial(kernel, dims), out_shape=(jax.ShapeDtype...]
where the time goes in v4:
time: 213 us; the launch traced here: 210 us
  Pallas kernels  209 us (98%)
    pallas_call x1, Pallas kernels, per_device(): pl.pallas_call(functools.partial(kernel, dims), out_shape=(jax.ShapeDtype...  200 us
    pallas_call x1, Pallas kernels, per_device(): pl.pallas_call(combine, grid=(steps,), out_shape=(jax.ShapeDtypeStruct((t...  8.69 us

profile of v4, /device:TPU:0, one launch (start us, length us, event | category | flops | bytes accessed | tf_op | source)
XLA Modules:
  0.0 209.8 jit_solution(10294779557823501616)
XLA Ops:
  0.6 200.5 %ffn_backward.1 = (f32[128,1024]{1,0:T(8,128)}, bf16[5,1024,384]{2,1,0:T(8,128)(2,1)}, bf16[5,1024,384]{2,1,0:T(8,128)(2,1)}) custom-call(s32[128,1024]{1,0:T(8,128)} %codes.1, s32[8,128]{1,0:T(8,128)} %bitcast.2, s32[1,128]{1,0:T(1,128)} %bitcast.3, bf16[128,1024]{1,0:T(8,128)(2,1)} %cot.1, bf16[1024,640]{1,0:T(8,128)(2,1)} %wg.1, bf16[1024,640]{1,0:T(8,128)(2,1)} %wu.1, ...), custom_call_target="tpu_custom_call" | custom-call | tf_op jit(solution)/shard_map/ffn_backward/pallas_call | solution.py:584
  201.1 8.7 %combine.1 = (f32[128,1024]{1,0:T(8,128)}, f32[1024,640]{1,0:T(8,128)}, f32[1024,640]{1,0:T(8,128)}, f32[1024,640]{1,0:T(8,128)}) custom-call(bf16[5,1024,384]{2,1,0:T(8,128)(2,1)} %get-tuple-element.7.own, bf16[5,1024,384]{2,1,0:T(8,128)(2,1)} %get-tuple-element.8.got, f32[128,1024]{1,0:T(8,128)} %get-tuple-element.9.dx), custom_call_target="tpu_custom_call" | custom-call | tf_op jit(solution)/shard_map/combine/pallas_call | solution.py:628

commit v5 on v4

--- a/solution.py
+++ b/solution.py
@@ -52,10 +52,10 @@
 def kernel(
     dims,
     codes, scales, mask, cot, wg, wu, wo,
-    dx_out, own_out, got_out,
-    sl, wc, pb, r1, r2, guh, dx, acc, dws, dwr, relay, dxs, dxr, ybuf, y2, zbuf,
+    dx_out, dws, dwr,
+    sl, wc, pb, r1, r2, guh, dx, acc, relay, dxs, dxr, ybuf, y2, zbuf,
     w_sem, ag_s, ag_r, rs1_s, rs1_r, rs2_s, rs2_r, a1_s, a1_r, a2_s, a2_r,
-    p1_s, p1_r, p2_s, p2_r, own_sem, got_sem, dxc_s, dxc_r, y1_s, y1_r, y2_s, y2_r, z_s, z_r,
+    p1_s, p1_r, p2_s, p2_r, dxc_s, dxc_r, y1_s, y1_r, y2_s, y2_r, z_s, z_r,
 ):
     tb, dl, chunks = dims
     blk = 4 * tb
@@ -149,9 +149,16 @@
             weight_copy(j, m, src).wait()
 
     def place(u):
-        s = (u // 8 + 1) // 2
-        k = (1 - s) * (u // 2) + s * lax.rem(u, 4)
-        return (1 - s) * lax.rem(u, 2) + s * (u // 4), (1 - s) * k + s * (3 - k), k
+        if isinstance(u, int) and u < 3:
+            return u, 0, 0
+        late, whole = (u + 3) // 12, u // 12
+        first = (u - 3) // 2 + 1
+        k = lax.rem(u, 4)
+        return (
+            (1 - late) * lax.rem(u - 3, 2) + late * (u // 4),
+            (1 - late) * first + late * (4 - whole - k),
+            (1 - late) * first + late * k,
+        )
 
     def unit(u):
         return place(u)[:2]
@@ -300,16 +307,10 @@
             to_z(1 - k // 2),
         )
 
-    def own_copy(j):
-        return pltpu.make_async_copy(dws.at[j], own_out.at[j], own_sem.at[j])
-
-    def got_copy(j):
-        return pltpu.make_async_copy(dwr.at[j], got_out.at[j], got_sem.at[j])
-
     def stage_dw(u):
         j, b, k = place(u)
         where = pl.ds(pl.multiple_of(b * blk, blk), blk)
-        sums = acc.at[lax.rem(j, 2)]
+        sums = acc.at[lax.rem(j, 3)]
 
         def body(i, carry):
             q = lax.rem(i, 2) * 2 + i // 2
@@ -335,10 +336,6 @@
 
         lax.fori_loop(0, 4, body, 0)
 
-        @pl.when(k == 3)
-        def _():
-            own_copy(j).start()
-
     def stage_g(j):
         for k in (0, 2, 1, 3):
             with jax.named_scope("g_wait"):
@@ -349,7 +346,6 @@
         with jax.named_scope("e_wait"):
             for k in (0, 2, 1, 3):
                 p2(j, k).wait_recv()
-        got_copy(j).start()
 
     dx[...] = jnp.zeros_like(dx)
     acc[...] = jnp.zeros_like(acc)
@@ -372,8 +368,13 @@
             with jax.named_scope(f"{stage.__name__}_{u}"):
                 stage(u)
 
-    run(stage_f, 0, 1)
-    run(stage_r, 0, 1)
+    def finish(u):
+        run(stage_dx, u)
+        run(stage_dw, u)
+
+    run(stage_f, 0, 1, 2)
+    run(stage_r, 0, 1, 2)
+    run(stage_a, 0)
     with jax.named_scope("ag1"):
         arrived(3, slot(1, 1, 0), tb)
         gather(7, slot(1, 1, 0), slot(3, 1, 0), part, up)
@@ -381,23 +382,23 @@
         arrived(4, slot(2, 1, 0), tb)
         gather(8, slot(2, 1, 0) + part, slot(3, 1, 0) + part, part, down)
         to_core(5, 2, 1)
-    run(stage_a, 0, 1)
+    run(stage_a, 1)
     with jax.named_scope("ag2"):
         arrived(11, slot(1, 0, 1), tb)
         arrived(13, slot(1, 1, 1), tb)
         arrived(12, slot(2, 0, 1), tb)
         arrived(14, slot(2, 1, 1), tb)
-    run(stage_f, 2, 3)
+    run(stage_f, 3, 4, 5, 6)
+    run(stage_a, 2)
     run(stage_w, 0, 1)
-    run(stage_f, 4, 5)
-    run(stage_r, 2, 3)
-    run(stage_dx, 0)
-    run(stage_dw, 0)
-    run(stage_a, 2)
-    run(stage_r, 4)
+    run(stage_r, 3, 4)
+    run(stage_w, 2)
+    finish(0)
+    finish(1)
     run(stage_a, 3)
     run(stage_r, 5)
-    run(stage_w, 2)
+    run(stage_a, 4)
+    run(stage_w, 3)
     with jax.named_scope("ag3"):
         arrived(5, slot(3, 0, 0), part)
         arrived(6, slot(3, 0, 0) + part, part)
@@ -407,17 +408,12 @@
         to_core(7, 3, 1)
         arrived(15, slot(3, 0, 1), tb)
         arrived(16, slot(3, 1, 1), tb)
-    run(stage_f, 6, 7)
-    run(stage_a, 4)
-    run(stage_w, 3)
+    run(stage_f, 7)
     run(stage_r, 6)
+    finish(2)
     run(stage_a, 5)
-    run(stage_dx, 1)
-    run(stage_dw, 1)
     run(stage_w, 4)
-    for u in (2, 3):
-        run(stage_dx, u)
-        run(stage_dw, u)
+    finish(3)
 
     last = chunks - 1
 
@@ -441,11 +437,11 @@
         at(4, stage_dx)
         at(4, stage_dw)
 
-        @pl.when(t >= 13)
+        @pl.when(t >= 14)
         def _():
             at_end(7, stage_g)
 
-        @pl.when(t >= 16)
+        @pl.when(t >= 17)
         def _():
             at_end(10, stage_e)
 
@@ -478,13 +474,17 @@
 
     def ring_early(way):
         b, zr = 2 - way, 1 - way
-        with jax.named_scope("core_wait"):
-            core_copy(b).wait()
+        if way == 0:
+            with jax.named_scope("core_wait"):
+                core_copy(b).wait()
         dxs[b, zr] = chip_sum(b, zr).astype(BF16)
         y2_copy(way, zr).start()
 
     def ring_late(way):
         b, zr = 2 - way, way
+        if way == 1:
+            with jax.named_scope("core_wait"):
+                core_copy(b).wait()
         with jax.named_scope("y1_wait"):
             y1_copy(zr).wait_recv()
         dxs[b, zr] = (chip_sum(b, zr) + ybuf[zr].astype(F32)).astype(BF16)
@@ -495,27 +495,27 @@
     run(stage_w, units - 3)
     run(stage_dx, units - 4)
     send_core(3)
-    run(stage_dw, units - 4)
     run(stage_a, units - 1)
     run(stage_w, units - 2)
+    run(stage_dw, units - 4)
     core_copy(3).wait()
     for zr in range(2):
         dxs[3, zr] = chip_sum(3, zr).astype(BF16)
         y1_copy(zr).start()
-    run(stage_g, last - 1)
     run(stage_dx, units - 3)
     send_core(2)
     run(stage_dw, units - 3)
     run(stage_w, units - 1)
-    ring_early(0)
+    run(stage_g, last - 1)
     run(stage_dx, units - 2)
     send_core(1)
+    ring_early(0)
     run(stage_dw, units - 2)
+    ring_late(1)
     run(arrive_dx, units - 1)
     run(stage_dw, units - 1)
     ring_early(1)
     ring_late(0)
-    ring_late(1)
     run(add_dx, units - 1)
     send_core(0)
     core_copy(0).wait()
@@ -528,13 +528,15 @@
     total = dx[dx_rows(0, 1, 0), :] + y2[0, 1].astype(F32) + y2[1, 1].astype(F32)
     dxs[0, 1] = total.astype(BF16)
     z_copy.start()
-    run(stage_e, last - 2)
-    for way in range(2):
-        y2_copy(way, 0).wait_recv()
+    with jax.named_scope("g_last"):
+        stage_g(last)
+    with jax.named_scope("y2_wait"):
+        for way in range(2):
+            y2_copy(way, 0).wait_recv()
     dx[dx_rows(0, 0, 0), :] = (
         dx[dx_rows(0, 0, 0), :] + y2[0, 0].astype(F32) + y2[1, 0].astype(F32)
     )
-    run(stage_g, last)
+    run(stage_e, last - 2)
     run(stage_e, last - 1)
     with jax.named_scope("z_wait"):
         z_copy.wait()
@@ -554,8 +556,6 @@
             for k in range(4):
                 p1(j, k).wait_send()
                 p2(j, k).wait_send()
-            own_copy(j).wait()
-            got_copy(j).wait()
         for zr in range(2):
             y1_copy(zr).wait_send()
             for way in range(2):
@@ -563,11 +563,15 @@
 
 
 def combine(own, got, dx, dx_out, g_out, u_out, o_out):
+    rows = g_out.shape[0]
+    where = pl.ds(pl.multiple_of(pl.program_id(0) * rows, rows), rows)
     for j in range(own.shape[0]):
         for m, out in enumerate((g_out, u_out, o_out)):
             lanes = pl.ds(m * W, W)
-            out[:, pl.ds(j * W, W)] = own[j, :, lanes].astype(F32) + got[j, :, lanes].astype(F32)
-    dx_out[...] = dx[...]
+            total = own[j, where, lanes].astype(F32) + got[j, where, lanes].astype(F32)
+            out[:, pl.ds(j * W, W)] = total
+    some = dx_out.shape[0]
+    dx_out[...] = dx[pl.ds(pl.multiple_of(pl.program_id(0) * some, some), some), :]
 
 
 def per_device(codes, scales, mask, cot, wg, wu, wo):
@@ -580,12 +584,12 @@
     vmem = pl.BlockSpec(memory_space=pltpu.VMEM)
     hbm = pl.BlockSpec(memory_space=pl.ANY)
     dma = pltpu.SemaphoreType.DMA
-    grads = jax.ShapeDtypeStruct((chunks, dl, 3 * W), BF16)
+    grads = pltpu.VMEM((chunks, dl, 3 * W), BF16)
     dx, own, got = pl.pallas_call(
         functools.partial(kernel, dims),
-        out_shape=(jax.ShapeDtypeStruct((tb, dl), F32), grads, grads),
+        out_shape=(pltpu.VMEM((tb, dl), F32), grads, grads),
         in_specs=[vmem] * 4 + [hbm] * 3,
-        out_specs=(vmem, hbm, hbm),
+        out_specs=(vmem, vmem, vmem),
         scratch_shapes=[
             pltpu.VMEM((16 * tb, 2 * dl), BF16),
             pltpu.VMEM((chunks, dl, 3 * W), BF16),
@@ -594,9 +598,7 @@
             pltpu.VMEM((units, 2, tile, 3 * W), jnp.int16),
             pltpu.VMEM((chunks, 16 * tb, 3 * W), BF16),
             pltpu.VMEM((16 * tb, dl), F32),
-            pltpu.VMEM((2, dl, 3 * W), F32),
-            pltpu.VMEM((chunks, dl, 3 * W), BF16),
-            pltpu.VMEM((chunks, dl, 3 * W), BF16),
+            pltpu.VMEM((3, dl, 3 * W), F32),
             pltpu.VMEM((chunks, dl, 3 * W), BF16),
             pltpu.VMEM((4, 2, tb, dl), BF16),
             pltpu.VMEM((4, 2, tb, dl), BF16),
@@ -611,14 +613,13 @@
             dma((units,)), dma((units,)),
             dma((chunks, 4)), dma((chunks, 4)),
             dma((chunks, 4)), dma((chunks, 4)),
-            dma((chunks,)), dma((chunks,)),
             dma((4,)), dma((4,)),
             dma((2,)), dma((2,)),
             dma((2, 2)), dma((2, 2)),
             dma((1,)), dma((1,)),
         ],
         compiler_params=pltpu.CompilerParams(
-            collective_id=0, has_side_effects=True, vmem_limit_bytes=67043328
+            collective_id=0, has_side_effects=True, vmem_limit_bytes=57671680
         ),
         name="ffn_backward",
     )(codes, scales.T, mask[None, :], cot, wg, wu, wo)
@@ -629,13 +630,10 @@
         combine,
         grid=(steps,),
         out_shape=(jax.ShapeDtypeStruct((tb, dl), F32), weight, weight, weight),
-        in_specs=[
-            pl.BlockSpec((chunks, rows, 3 * W), lambda i: (0, i, 0)),
-            pl.BlockSpec((chunks, rows, 3 * W), lambda i: (0, i, 0)),
-            pl.BlockSpec((tb // steps, dl), lambda i: (i, 0)),
-        ],
+        in_specs=[vmem] * 3,
         out_specs=[pl.BlockSpec((tb // steps, dl), lambda i: (i, 0))]
         + [pl.BlockSpec((rows, fl), lambda i: (i, 0))] * 3,
+        compiler_params=pltpu.CompilerParams(vmem_limit_bytes=24 * 1024 * 1024),
         name="combine",
     )(own, got, dx)
 

time: 213 us -> 206 us (0.967)
  Pallas kernels: 209 us -> 204 us
    pallas_call x1, Pallas kernels: 8.69 us -> 4.37 us  [per_device(): pl.pallas_call(combine, grid=(steps,), out_shape=(jax.ShapeDtypeStruct((t...]
where the time goes in v5:
time: 206 us; the launch traced here: 204 us
  Pallas kernels  204 us (99%)
    pallas_call x1, Pallas kernels, per_device(): pl.pallas_call(functools.partial(kernel, dims), out_shape=(pltpu.VMEM((tb...  199 us
    pallas_call x1, Pallas kernels, per_device(): pl.pallas_call(combine, grid=(steps,), out_shape=(jax.ShapeDtypeStruct((t...  4.37 us

profile of v5, /device:TPU:0, one launch (start us, length us, event | category | flops | bytes accessed | tf_op | source)
XLA Modules:
  0.0 204.2 jit_solution(5076316861359926845)
XLA Ops:
  0.6 199.2 %ffn_backward.1 = (f32[128,1024]{1,0:T(8,128)S(1)}, bf16[5,1024,384]{2,1,0:T(8,128)(2,1)S(1)}, bf16[5,1024,384]{2,1,0:T(8,128)(2,1)S(1)}) custom-call(s32[128,1024]{1,0:T(8,128)} %codes.1, s32[8,128]{1,0:T(8,128)} %bitcast.2, s32[1,128]{1,0:T(1,128)} %bitcast.3, bf16[128,1024]{1,0:T(8,128)(2,1)} %cot.1, bf16[1024,640]{1,0:T(8,128)(2,1)} %wg.1, ...), custom_call_target="tpu_custom_call" | custom-call | tf_op jit(solution)/shard_map/ffn_backward/pallas_call | solution.py:588
  199.9 4.4 %combine.1 = (f32[128,1024]{1,0:T(8,128)}, f32[1024,640]{1,0:T(8,128)}, f32[1024,640]{1,0:T(8,128)}, f32[1024,640]{1,0:T(8,128)}) custom-call(bf16[5,1024,384]{2,1,0:T(8,128)(2,1)S(1)} %get-tuple-element.7.own, bf16[5,1024,384]{2,1,0:T(8,128)(2,1)S(1)} %get-tuple-element.8.got, f32[128,1024]{1,0:T(8,128)S(1)} %get-tuple-element.9.dx), custom_call_target="tpu_custom_call" | custom-call | tf_op jit(solution)/shard_map/combine/pallas_call | solution.py:629

commit v6 on v5

--- a/solution.py
+++ b/solution.py
@@ -185,10 +185,10 @@
     def a2(u, owner):
         j, b = unit(u)
         ref = grad_rows(j, b, owner)
-        return remote(ref, ref, a2_s.at[u], a2_r.at[u], to_row(lax.rem(b, 2)))
+        return remote(ref, ref, a2_s.at[u], a2_r.at[u], to_row(lax.rem(u, 2)))
 
     def sent(u):
-        rs1(u, lax.rem(unit(u)[1], 2)).wait_send()
+        rs1(u, lax.rem(u, 2)).wait_send()
         for way in range(2):
             rs2(u, way).wait_send()
 
@@ -210,11 +210,11 @@
             tile = held(u).at[o]
             store_coded(tile, pl.ds(0, 2 * W), both[o * tb : (o + 1) * tb])
             store_coded(tile, pl.ds(2 * W, W), back[o * tb : (o + 1) * tb])
-        rs1(u, lax.rem(b, 2)).start()
+        rs1(u, lax.rem(u, 2)).start()
 
     def stage_r(u):
         j, b = unit(u)
-        way = lax.rem(b, 2)
+        way = lax.rem(u, 2)
         rs2(u, 1 - way).start()
         with jax.named_scope("r_wait"):
             rs1(u, way).wait_recv()
@@ -262,15 +262,14 @@
             a1(u, way, x).start()
 
     def stage_w(u):
-        b = unit(u)[1]
-        way = lax.rem(b, 2)
+        way = lax.rem(u, 2)
         with jax.named_scope("w_wait"):
             a1(u, way, beside(1 - way)).wait_recv()
         a2(u, beside(1 - way)).start()
 
     def arrive_dx(u):
         j, b = unit(u)
-        way = lax.rem(b, 2)
+        way = lax.rem(u, 2)
         with jax.named_scope("b_wait"):
             a1(u, 1 - way, beside(way)).wait_recv()
             a2(u, opp).wait_recv()

time: 206 us -> 197 us (0.956)
  Pallas kernels: 204 us -> 196 us
    pallas_call x1, Pallas kernels: 199 us -> 192 us  [per_device(): pl.pallas_call(functools.partial(kernel, dims), out_shape=(pltpu.VMEM((tb...]
where the time goes in v6:
time: 197 us
  Pallas kernels  196 us (99%)
    pallas_call x1, Pallas kernels, per_device(): pl.pallas_call(functools.partial(kernel, dims), out_shape=(pltpu.VMEM((tb...  192 us
    pallas_call x1, Pallas kernels, per_device(): pl.pallas_call(combine, grid=(steps,), out_shape=(jax.ShapeDtypeStruct((t...  4.37 us

profile of v6, /device:TPU:0, one launch (start us, length us, event | category | flops | bytes accessed | tf_op | source)
XLA Modules:
  0.0 197.1 jit_solution(15630270026657501449)
XLA Ops:
  0.6 192.1 %ffn_backward.1 = (f32[128,1024]{1,0:T(8,128)S(1)}, bf16[5,1024,384]{2,1,0:T(8,128)(2,1)S(1)}, bf16[5,1024,384]{2,1,0:T(8,128)(2,1)S(1)}) custom-call(s32[128,1024]{1,0:T(8,128)} %codes.1, s32[8,128]{1,0:T(8,128)} %bitcast.2, s32[1,128]{1,0:T(1,128)} %bitcast.3, bf16[128,1024]{1,0:T(8,128)(2,1)} %cot.1, bf16[1024,640]{1,0:T(8,128)(2,1)} %wg.1, ...), custom_call_target="tpu_custom_call" | custom-call | tf_op jit(solution)/shard_map/ffn_backward/pallas_call | solution.py:587
  192.7 4.4 %combine.1 = (f32[128,1024]{1,0:T(8,128)}, f32[1024,640]{1,0:T(8,128)}, f32[1024,640]{1,0:T(8,128)}, f32[1024,640]{1,0:T(8,128)}) custom-call(bf16[5,1024,384]{2,1,0:T(8,128)(2,1)S(1)} %get-tuple-element.7.own, bf16[5,1024,384]{2,1,0:T(8,128)(2,1)S(1)} %get-tuple-element.8.got, f32[128,1024]{1,0:T(8,128)S(1)} %get-tuple-element.9.dx), custom_call_target="tpu_custom_call" | custom-call | tf_op jit(solution)/shard_map/combine/pallas_call | solution.py:628

commit v7 on v6

--- a/solution.py
+++ b/solution.py
@@ -440,10 +440,6 @@
         def _():
             at_end(7, stage_g)
 
-        @pl.when(t >= 17)
-        def _():
-            at_end(10, stage_e)
-
         return carry
 
     lax.fori_loop(8, units, step, 0)
@@ -510,9 +506,9 @@
     send_core(1)
     ring_early(0)
     run(stage_dw, units - 2)
-    ring_late(1)
     run(arrive_dx, units - 1)
     run(stage_dw, units - 1)
+    ring_late(1)
     ring_early(1)
     ring_late(0)
     run(add_dx, units - 1)
@@ -535,8 +531,8 @@
     dx[dx_rows(0, 0, 0), :] = (
         dx[dx_rows(0, 0, 0), :] + y2[0, 0].astype(F32) + y2[1, 0].astype(F32)
     )
-    run(stage_e, last - 2)
-    run(stage_e, last - 1)
+    for j in range(last):
+        run(stage_e, j)
     with jax.named_scope("z_wait"):
         z_copy.wait()
     dx_out[...] = dx[dx_rows(0, 0, 0), :] + zbuf[...].astype(F32)

time: 197 us -> 197 us (level)
  no operation moved by 1% of the time
where the time goes in v7:
time: 197 us
  Pallas kernels  196 us (99%)
    pallas_call x1, Pallas kernels, per_device(): pl.pallas_call(functools.partial(kernel, dims), out_shape=(pltpu.VMEM((tb...  192 us
    pallas_call x1, Pallas kernels, per_device(): pl.pallas_call(combine, grid=(steps,), out_shape=(jax.ShapeDtypeStruct((t...  4.37 us

profile of v7, /device:TPU:0, one launch (start us, length us, event | category | flops | bytes accessed | tf_op | source)
XLA Modules:
  0.0 197.1 jit_solution(17344177924437968106)
XLA Ops:
  0.6 192.1 %ffn_backward.1 = (f32[128,1024]{1,0:T(8,128)S(1)}, bf16[5,1024,384]{2,1,0:T(8,128)(2,1)S(1)}, bf16[5,1024,384]{2,1,0:T(8,128)(2,1)S(1)}) custom-call(s32[128,1024]{1,0:T(8,128)} %codes.1, s32[8,128]{1,0:T(8,128)} %bitcast.2, s32[1,128]{1,0:T(1,128)} %bitcast.3, bf16[128,1024]{1,0:T(8,128)(2,1)} %cot.1, bf16[1024,640]{1,0:T(8,128)(2,1)} %wg.1, ...), custom_call_target="tpu_custom_call" | custom-call | tf_op jit(solution)/shard_map/ffn_backward/pallas_call | solution.py:583
  192.7 4.4 %combine.1 = (f32[128,1024]{1,0:T(8,128)}, f32[1024,640]{1,0:T(8,128)}, f32[1024,640]{1,0:T(8,128)}, f32[1024,640]{1,0:T(8,128)}) custom-call(bf16[5,1024,384]{2,1,0:T(8,128)(2,1)S(1)} %get-tuple-element.7.own, bf16[5,1024,384]{2,1,0:T(8,128)(2,1)S(1)} %get-tuple-element.8.got, f32[128,1024]{1,0:T(8,128)S(1)} %get-tuple-element.9.dx), custom_call_target="tpu_custom_call" | custom-call | tf_op jit(solution)/shard_map/combine/pallas_call | solution.py:624
